TPU v7x, 256 devices: a whole 4x4x8 slice. The times are simulated.
256 devices in a mesh: dp: 64 (over z, y, core), tp: 4 (over x).
Axes of the slice: x: 4, y: 4, z: 8, core: 2. Of those that a mesh axis runs over, the one named last changes fastest.
Arguments:
- irreps: bfloat16 [131072, 9, 128], P('dp', None, 'tp')
- norm_gain: float32 [3, 128], P(None, 'tp')
- w_up: bfloat16 [3, 128, 512], P(None, None, 'tp')
- w_gate: bfloat16 [128, 512], P(None, 'tp')
- w_down: bfloat16 [3, 512, 128], P(None, 'tp')
- to_grid: float32 [9, 36], replicated
- from_grid: float32 [36, 8], replicated
- grad_out: bfloat16 [131072, 9, 128], P('dp', None, 'tp')
Outputs:
- output 1: bfloat16 [131072, 9, 128], P('dp', None, 'tp')
- output 2: bfloat16 [131072, 9, 128], P('dp', None, 'tp')
- output 3: bfloat16 [3, 128, 512], P(None, None, 'tp')
- output 4: bfloat16 [128, 512], P(None, 'tp')
- output 5: bfloat16 [3, 512, 128], P(None, 'tp')
All inputs are finite; a program needn't handle non-finite values.
Results may differ from a plain program's by a relative error of at most 0.0120943.
Values are sent between devices in bfloat16 or wider.
A program may use at most 768 MiB of HBM per device.

v0:
```python
import math
import jax
import jax.numpy as jnp
from jax import lax
from jax.sharding import PartitionSpec as P

NORM_EPS = 1e-5


def expand_rows(per_degree):
    return jnp.concatenate([jnp.broadcast_to(per_degree[degree:degree + 1], (2 * degree + 1,) + per_degree.shape[1:]) for degree in range(per_degree.shape[0])], axis=0)


def degree_sums(per_coef):
    degrees = math.isqrt(per_coef.shape[0])
    return jnp.stack([per_coef[degree * degree:(degree + 1) * (degree + 1)].sum(axis=0) for degree in range(degrees)], axis=0)


def silu_grad(pre_act):
    sig_val = jax.nn.sigmoid(pre_act)
    return sig_val * (1.0 + pre_act * (1.0 - sig_val))


def hidden_block(xn_blk, grad_blk, up_rows, gate_loc, down_rows, grid_in, grid_back):
    hidden_act = jnp.einsum('nkc,kch->nkh', xn_blk, up_rows, preferred_element_type=jnp.float32).astype(jnp.bfloat16)
    pre_gate = jnp.dot(xn_blk[:, 0, :], gate_loc, preferred_element_type=jnp.float32).astype(jnp.bfloat16)
    gate_pre_f = pre_gate.astype(jnp.float32)
    gate_val = jax.nn.silu(gate_pre_f).astype(jnp.bfloat16)
    pre_grid = jnp.einsum('nkh,kg->ngh', hidden_act, grid_in, preferred_element_type=jnp.float32).astype(jnp.bfloat16)
    grid_pre_f = pre_grid.astype(jnp.float32)
    grid_val = jax.nn.silu(grid_pre_f).astype(jnp.bfloat16)
    back_proj = jnp.einsum('ngh,gk->nkh', grid_val, grid_back, preferred_element_type=jnp.float32).astype(jnp.bfloat16)
    mixed_act = jnp.concatenate([gate_val[:, None, :], back_proj], axis=1)
    part_out = jnp.einsum('nkh,khc->nkc', mixed_act, down_rows, preferred_element_type=jnp.float32).astype(jnp.bfloat16)
    d_mixed = jnp.einsum('nkc,khc->nkh', grad_blk, down_rows, preferred_element_type=jnp.float32).astype(jnp.bfloat16)
    g_down = jnp.einsum('nkh,nkc->khc', mixed_act, grad_blk, preferred_element_type=jnp.float32)
    d_grid = jnp.einsum('nkh,gk->ngh', d_mixed[:, 1:, :], grid_back, preferred_element_type=jnp.float32).astype(jnp.bfloat16)
    d_pre_grid = (d_grid.astype(jnp.float32) * silu_grad(grid_pre_f)).astype(jnp.bfloat16)
    d_hidden = jnp.einsum('ngh,kg->nkh', d_pre_grid, grid_in, preferred_element_type=jnp.float32).astype(jnp.bfloat16)
    d_pre_gate = (d_mixed[:, 0, :].astype(jnp.float32) * silu_grad(gate_pre_f)).astype(jnp.bfloat16)
    g_up = jnp.einsum('nkc,nkh->kch', xn_blk, d_hidden, preferred_element_type=jnp.float32)
    g_gate = jnp.einsum('nc,nh->ch', xn_blk[:, 0, :], d_pre_gate, preferred_element_type=jnp.float32)
    d_xn = jnp.einsum('nkh,kch->nkc', d_hidden, up_rows, preferred_element_type=jnp.float32)
    d_xn_zero = d_xn[:, 0, :] + jnp.einsum('nh,ch->nc', d_pre_gate, gate_loc, preferred_element_type=jnp.float32)
    d_xn = jnp.concatenate([d_xn_zero[:, None, :], d_xn[:, 1:, :]], axis=1).astype(jnp.bfloat16)
    return part_out, d_xn, g_up, g_gate, g_down


def hidden_pass(xn_full, grad_full, up_loc, gate_loc, down_loc, to_grid, from_grid):
    node_count, coef_count, channels = xn_full.shape
    blk_rows = math.gcd(node_count, 128)
    blk_count = node_count // blk_rows
    up_rows = expand_rows(up_loc)
    down_rows = expand_rows(down_loc)
    grid_in = to_grid.astype(jnp.bfloat16)
    grid_back = from_grid.astype(jnp.bfloat16)

    def scan_step(grad_sums, blk_pair):
        part_out, d_xn, g_up, g_gate, g_down = hidden_block(blk_pair[0], blk_pair[1], up_rows, gate_loc, down_rows, grid_in, grid_back)
        return (grad_sums[0] + g_up, grad_sums[1] + g_gate, grad_sums[2] + g_down), (part_out, d_xn)

    init_sums = (jnp.zeros(up_rows.shape, jnp.float32), jnp.zeros(gate_loc.shape, jnp.float32), jnp.zeros(down_rows.shape, jnp.float32))
    blk_shape = (blk_count, blk_rows, coef_count, channels)
    total_sums, (part_outs, d_xns) = lax.scan(scan_step, init_sums, (xn_full.reshape(blk_shape), grad_full.reshape(blk_shape)))
    full_shape = (node_count, coef_count, channels)
    return part_outs.reshape(full_shape), d_xns.reshape(full_shape), degree_sums(total_sums[0]), total_sums[1], degree_sums(total_sums[2])


def solution(mesh):
    tp_size = mesh.shape['tp']
    act_spec = P('dp', None, 'tp')
    in_specs = (act_spec, P(None, 'tp'), P(None, None, 'tp'), P(None, 'tp'), P(None, 'tp', None), P(None, None), P(None, None), act_spec)
    out_specs = (act_spec, act_spec, P(None, None, 'tp'), P(None, 'tp'), P(None, 'tp', None))

    def local_step(x_loc, gain_loc, up_loc, gate_loc, down_loc, to_grid, from_grid, grad_loc):
        coef_count = x_loc.shape[1]
        channels = x_loc.shape[2] * tp_size
        vec_count = channels * (coef_count - 1)
        x_f = x_loc.astype(jnp.float32)
        scalar = x_f[:, 0, :]
        vector = x_f[:, 1:, :]
        node_stats = jnp.stack([jnp.sum(scalar, axis=-1), jnp.sum(scalar * scalar, axis=-1), jnp.sum(vector * vector, axis=(1, 2))], axis=-1)
        node_stats = lax.psum(node_stats, 'tp')
        mean_s = node_stats[:, 0:1] / channels
        inv_s = lax.rsqrt(node_stats[:, 1:2] / channels - mean_s * mean_s + NORM_EPS)
        inv_v = lax.rsqrt(node_stats[:, 2] / vec_count + NORM_EPS)[:, None, None]
        hat_s = (scalar - mean_s) * inv_s
        hat_v = vector * inv_v
        gain_rows = expand_rows(gain_loc)
        xn_loc = jnp.concatenate([(hat_s * gain_rows[0])[:, None, :], hat_v * gain_rows[1:]], axis=1).astype(jnp.bfloat16)
        xn_full = lax.all_gather(xn_loc, 'tp', axis=2, tiled=True)
        grad_full = lax.all_gather(grad_loc, 'tp', axis=2, tiled=True)
        part_out, d_xn_part, g_up, g_gate, g_down = hidden_pass(xn_full, grad_full, up_loc, gate_loc, down_loc, to_grid, from_grid)
        ffn_delta = lax.psum_scatter(part_out, 'tp', scatter_dimension=2, tiled=True)
        out_loc = (x_f + ffn_delta.astype(jnp.float32)).astype(jnp.bfloat16)
        d_norm = lax.psum_scatter(d_xn_part, 'tp', scatter_dimension=2, tiled=True).astype(jnp.float32)
        d_hat_s = d_norm[:, 0, :] * gain_rows[0]
        d_hat_v = d_norm[:, 1:, :] * gain_rows[1:]
        back_stats = jnp.stack([jnp.sum(d_hat_s, axis=-1), jnp.sum(d_hat_s * hat_s, axis=-1), jnp.sum(d_hat_v * vector, axis=(1, 2))], axis=-1)
        back_stats = lax.psum(back_stats, 'tp')
        dx_s = inv_s * (d_hat_s - back_stats[:, 0:1] / channels - hat_s * back_stats[:, 1:2] / channels)
        dx_v = inv_v * d_hat_v - vector * (inv_v ** 3) * (back_stats[:, 2] / vec_count)[:, None, None]
        d_irreps = (jnp.concatenate([dx_s[:, None, :], dx_v], axis=1) + grad_loc.astype(jnp.float32)).astype(jnp.bfloat16)
        d_up = lax.psum(g_up, 'dp').astype(jnp.bfloat16)
        d_gate = lax.psum(g_gate, 'dp').astype(jnp.bfloat16)
        d_down = lax.psum(g_down, 'dp').astype(jnp.bfloat16)
        return out_loc, d_irreps, d_up, d_gate, d_down

    return jax.shard_map(local_step, mesh=mesh, in_specs=in_specs, out_specs=out_specs, check_vma=False)
```

profile of v0, /device:TPU:4, one launch (start us, length us, event | category | flops | bytes accessed | tf_op | source)
XLA Modules:
  0.0 817.0 jit_solution(15960523951363959567)
XLA Ops:
  9.1 15.5 %psum.35 = f32[2048,3]{0,1:T(4,128)S(1)} all-reduce(f32[2048,3]{0,1:T(4,128)S(1)} %pad_maximum_fusion.6), channel_id=1, replica_groups=mesh['dp'=64,'tp'=4] {'tp'}, use_global_device_ids=true, to_apply=%region_3.0 | all-reduce | flops 6144 | bytes 49152 | tf_op jit(solution)/shard_map/psum | solution.py:83
  28.9 54.9 %all-gather.3.cloned.1.call-done = bf16[2048,9,128]{0,2,1:T(8,128)(2,1)} async-done(((bf16[2048,9,32]{0,2,1:T(8,128)(2,1)}), bf16[2048,9,128]{0,2,1:T(8,128)(2,1)}) %all-gather.3.cloned.1.call-update) | async-done | bytes 4718608 | tf_op jit(solution)/shard_map/all_gather | solution.py:91
  83.8 6.1 copy.46
  89.9 7.0 copy.40
  96.8 44.3 %all-gather.5.cloned.1.call-done = bf16[2048,9,128]{0,2,1:T(8,128)(2,1)} async-done(((bf16[2048,9,32]{0,2,1:T(8,128)(2,1)}), bf16[2048,9,128]{0,2,1:T(8,128)(2,1)}) %all-gather.5.cloned.1.call-update) | async-done | bytes 4718608 | tf_op jit(solution)/shard_map/all_gather | solution.py:92
  141.1 6.6 copy.39
  147.8 351.1 %while.19 = (s32[]{:T(128)}, f32[9,128,128]{2,1,0:T(8,128)}, f32[128,128]{1,0:T(8,128)}, f32[9,128,128]{2,1,0:T(8,128)}, bf16[16,128,9,128]{3,1,2,0:T(8,128)(2,1...) while((s32[]{:T(128)}, f32[9,128,128]{2,1,0:T(8,128)}, ...), condition=%wide.region_5.6_spmd.clone, body=%wide.region_4.5_spmd.clone.sunk | while | flops 293388288 | bytes 22057628 | solution.py:64
  152.9 3.7 fusion.128
  174.5 3.7 fusion.128
  196.5 3.7 fusion.128
  208.5 2.3 convolution_add_fusion.7
  218.4 3.7 fusion.128
  230.4 2.3 convolution_add_fusion.7
  240.4 3.7 fusion.128
  262.4 3.7 fusion.128
  284.4 3.7 fusion.128
  306.3 3.7 fusion.128
  328.3 3.7 fusion.128
  350.3 3.7 fusion.128
  372.2 3.7 fusion.128
  394.2 3.7 fusion.128
  416.1 3.7 fusion.128
  438.1 3.7 fusion.128
  460.1 3.7 fusion.128
  482.1 3.7 fusion.128
  498.9 7.0 copy.43
  505.9 8.2 %reshape.144 = bf16[2048,9,128]{0,2,1:T(8,128)(2,1)} reshape(bf16[16,128,9,128]{1,0,3,2:T(8,128)(2,1)} %copy.43) | data formatting | bytes 9437184 | tf_op jit(solution)/shard_map/reshape | solution.py:66
  514.2 7.0 copy.42
  521.2 8.2 %reshape.143 = bf16[2048,9,128]{0,2,1:T(8,128)(2,1)} reshape(bf16[16,128,9,128]{1,0,3,2:T(8,128)(2,1)} %copy.42) | data formatting | bytes 9437184 | tf_op jit(solution)/shard_map/reshape | solution.py:66
  530.8 254.4 %all-reduce.2 = (bf16[3,128,128]{2,1,0:T(8,128)(2,1)}, bf16[128,128]{1,0:T(8,128)(2,1)}, bf16[3,128,128]{2,1,0:T(8,128)(2,1)}) all-reduce(f32[3,128,128]{2,1,0:T(8,128)S(1)} %pad_maximum_fusion.4, f32[128,128]{1,0:T(8,128)} %get-tuple-element.79, f32[3,128,128]{2,1,0:T(8,128)S(1)} %pad_maximum_fusion.5), channel_id=1, replica_groups=mesh['dp'=64,'tp'=4] {'dp'}, use_global_device_ids=true, to_apply=%region_14.15 | all-reduce | flops 114688 | bytes 688128 | tf_op jit(solution)/shard_map/psum | solution.py:104
  788.2 14.8 %psum.36 = f32[2048,3]{0,1:T(4,128)S(1)} all-reduce(f32[2048,3]{0,1:T(4,128)S(1)} %pad_maximum_fusion.7), channel_id=1, replica_groups=mesh['dp'=64,'tp'=4] {'tp'}, use_global_device_ids=true, to_apply=%region_11.12 | all-reduce | flops 6144 | bytes 49152 | tf_op jit(solution)/shard_map/psum | solution.py:100
  807.7 2.7 add_convert_fusion
  (502 shorter events, 300.8 us)
Async XLA Ops:
  7.2 17.5 %copy-start.20 = (f32[3,32]{1,0:T(4,128)S(1)}, f32[3,32]{1,0:T(4,128)}, u32[]{:S(2)}) copy-start(f32[3,32]{1,0:T(4,128)} %param.11) | copy-start | bytes 1156
  7.2 76.6 %all-gather.3.cloned.1.call-start = ((), (), s32[]{:S(2)}) async-start(), calls=%async_computation.2 | async-start | bytes 5898240 | tf_op jit(solution)/shard_map/all_gather | solution.py:91
  26.5 114.6 %all-gather.5.cloned.1.call-start = ((), (), s32[]{:S(2)}) async-start(), calls=%async_computation.3 | async-start | bytes 5898240 | tf_op jit(solution)/shard_map/all_gather | solution.py:92
  27.3 757.9 %reduce-scatter.5.cloned.1.call-start = ((), (), s32[]{:S(2)}) async-start(), calls=%async_computation.5 | async-start | bytes 5898240 | tf_op jit(solution)/shard_map/reduce_scatter | solution.py:96
  152.9 6.2 copy-start.1
  174.5 6.2 copy-start.1
  184.1 4.7 copy-start.13
  196.4 6.2 copy-start.1
  206.1 4.7 copy-start.13
  218.4 6.2 copy-start.1
  228.1 4.7 copy-start.13
  240.4 6.2 copy-start.1
  262.3 6.2 copy-start.1
  284.3 6.2 copy-start.1
  306.3 6.2 copy-start.1
  316.0 4.7 copy-start.13
  328.2 6.2 copy-start.1
  337.9 4.7 copy-start.13
  350.2 6.2 copy-start.1
  372.2 6.2 copy-start.1
  381.9 4.7 copy-start.13
  394.1 6.2 copy-start.1
  416.1 6.2 copy-start.1
  425.8 4.7 copy-start.13
  438.1 6.2 copy-start.1
  460.1 6.2 copy-start.1
  482.0 6.2 copy-start.1
  514.1 293.6 %reduce-scatter.3.cloned.1.call-start = ((), (), s32[]{:S(2)}) async-start(), calls=%async_computation.4 | async-start | bytes 5898240 | tf_op jit(solution)/shard_map/reduce_scatter | solution.py:94
  530.7 256.0 %copy-start.18 = (f32[32]{0:T(128)S(1)}, f32[32]{0:T(128)}, u32[]{:S(2)}) copy-start(f32[32]{0:T(128)} %copy-done.17) | copy-start | bytes 388
  530.7 256.0 %copy-start.8 = (f32[2048,1]{0,1:T(1,128)S(1)}, f32[2048,1]{0,1:T(1,128)}, u32[]{:S(2)}) copy-start(f32[2048,1]{0,1:T(1,128)} %copy-done.7) | copy-start | bytes 24580
  530.7 256.0 %copy-start.10 = (f32[2048,1]{0,1:T(1,128)S(1)}, f32[2048,1]{0,1:T(1,128)}, u32[]{:S(2)}) copy-start(f32[2048,1]{0,1:T(1,128)} %copy-done.9) | copy-start | bytes 24580
  786.8 17.3 %copy-start.15 = (f32[2048]{0:T(1024)S(1)}, f32[2048]{0:T(1024)}, u32[]{:S(2)}) copy-start(f32[2048]{0:T(1024)} %multiply_multiply_fusion) | copy-start | bytes 24580
  (53 other events, 136.7 us)
Sparse Core Ops, SparseCore 0:
  26.6 57.1 all-gather.2
  85.6 55.4 all-gather.4
  514.3 53.3 reduce-scatter.4
  570.1 53.3 reduce-scatter.2
where the time goes:
time: 825 us; the launch traced here: 817 us
  matrix products  307 us (37%)
  blocking collectives  285 us (35%)
  waiting for transfers between devices  100 us (12%)
  local copies, waits for them, and re-layouts  79.4 us (10%)
  other arithmetic  30.4 us (4%)
  between operations  14.2 us (2%)
    psum x1, blocking collectives, local_step(): d_up = lax.psum(g_up, 'dp').astype(jnp.bfloat16)  254 us
    dot_general x16, matrix products, hidden_block(): jnp.einsum('ngh,kg->nkh', d_pre_grid, grid_in, preferred_element_type=jnp...  59.1 us
    all_gather x1, waiting for transfers between devices, local_step(): xn_full = lax.all_gather(xn_loc, 'tp', axis=2, tiled=True)  54.9 us
    all_gather x1, waiting for transfers between devices, local_step(): grad_full = lax.all_gather(grad_loc, 'tp', axis=2, tiled=True)  44.3 us
    dot_general x16, matrix products, hidden_block(): jnp.einsum('nkc,nkh->kch', xn_blk, d_hidden, preferred_element_type=jnp.f...  37.2 us
    dot_general x16, matrix products, hidden_block(): jnp.einsum('nkh,nkc->khc', mixed_act, grad_blk, preferred_element_type=jn...  37.1 us
    dot_general x16, matrix products, hidden_block(): jnp.einsum('nkh,kg->ngh', hidden_act, grid_in, preferred_element_type=jnp...  25.8 us
    dot_general x16, matrix products, hidden_block(): jnp.einsum('nkh,kch->nkc', d_hidden, up_rows, preferred_element_type=jnp....  24.8 us
  transfers between devices with their start and end apart: 4, of which 2 were waited for; matrix products, arithmetic and copies ran while one was open for 5% of the time, Pallas kernels for 0%

commit v1 on v0

v1 whole, which is shorter than its diff:
```python
import functools
import jax
import jax.numpy as jnp
from jax import lax
from jax.experimental import pallas as pl
from jax.experimental.pallas import tpu as pltpu
from jax.sharding import PartitionSpec as P

NORM_EPS = 1e-5
COEFS = 9
CH = 128
HID = 512
SUB = 16
BLK = 256
GRID_ROWS = 576
GRID_PAD = 640
SLAB = 56
ROWS = 896
DEGS = 3
TP = 4
VMEM_LIMIT = 60 * 2**20
F32 = jnp.float32
BF16 = jnp.bfloat16


def iota(shape, axis):
    return lax.broadcasted_iota(jnp.int32, shape, axis)


def mm(a, b):
    return jnp.dot(a, b, preferred_element_type=F32)


def mm_nt(a, b):
    return lax.dot_general(a, b, (((1,), (1,)), ((), ())), preferred_element_type=F32)


def one_hot(shape, row_div, col_div):
    return jnp.where(iota(shape, 0) // row_div == iota(shape, 1) // col_div, 1.0, 0.0).astype(BF16)


def spread(table, rows, row_div, cols, col_div):
    left = mm(one_hot((rows, CH), row_div, 1), table).astype(BF16)
    full = mm(left, one_hot((CH, cols), 1, col_div))
    same = iota((rows, cols), 0) % SUB == iota((rows, cols), 1) % SUB
    return jnp.where(same, full, 0.0)


def degree_of(coef):
    return jnp.where(coef >= 4, 2, jnp.where(coef >= 1, 1, 0))


def setup_tables(tog_ref, frg_ref, kg, kf, kft, kgt):
    tog = tog_ref[...].astype(BF16)
    frg = frg_ref[...].astype(BF16)
    tog_t = tog_ref[...].T.astype(BF16)
    frg_t = frg_ref[...].T.astype(BF16)
    kg[...] = (0.5 * spread(tog_t, GRID_ROWS, SUB, BLK, SUB)).astype(BF16)
    kf[...] = (0.5 * spread(frg, GRID_ROWS, SUB, CH, SUB)).astype(BF16)
    kft[...] = spread(frg_t, CH, SUB, GRID_PAD, SUB).astype(BF16)
    kgt[...] = spread(tog, 144, SUB, GRID_PAD, SUB).astype(BF16)


def compute_block(lanes, x_ref, g_ref, gain_ref, wup, wgate, wdown, out_ref, dx_ref, grad_ref,
                  wup_t, wgate_t, wdown_t, kg, kf, kft, kgt, n_s, y_s, dm_s, m_s, dy_s, da_s, dn_s, s_bufs, du_bufs):
    gain = [jnp.concatenate([gain_ref[degree]] * 2, axis=1) for degree in range(DEGS)]
    x0 = x_ref[0, :, lanes].astype(F32)
    mean_s = jnp.sum(x0, axis=0, keepdims=True) * (1.0 / CH)
    cen = x0 - mean_s
    inv_s = lax.rsqrt(jnp.sum(cen * cen, axis=0, keepdims=True) * (1.0 / CH) + NORM_EPS)
    n_s[0] = ((cen * inv_s) * gain[0]).astype(BF16)
    acc = jnp.zeros((CH, BLK), F32)
    for coef in range(1, COEFS):
        xk = x_ref[coef, :, lanes].astype(F32)
        acc = acc + xk * xk
    inv_v = lax.rsqrt(jnp.sum(acc, axis=0, keepdims=True) * (1.0 / 1024) + NORM_EPS)
    for coef in range(1, COEFS):
        xk = x_ref[coef, :, lanes].astype(F32)
        n_s[coef] = ((xk * inv_v) * gain[1 if coef < 4 else 2]).astype(BF16)

    def up_step(coef, carry):
        degree = degree_of(coef)
        y_s[coef] = mm(wup_t[degree], n_s[coef]).astype(BF16)
        dm_s[coef] = mm(wdown[degree], g_ref[coef, :, lanes]).astype(BF16)
        return carry
    lax.fori_loop(0, COEFS, up_step, 0)

    def gate_step(i, carry):
        rows = pl.ds(pl.multiple_of(i * CH, CH), CH)
        half = (0.5 * mm(wgate_t[rows, :], n_s[0])).astype(BF16).astype(F32)
        th = jnp.tanh(half)
        plus = 1.0 + th
        val = half * plus
        m_s[0, rows, :] = val.astype(BF16)
        slope = 0.5 * (plus + val * (1.0 - th))
        da_s[rows, :] = (dm_s[0, rows, :].astype(F32) * slope).astype(BF16)
        return carry
    lax.fori_loop(0, 4, gate_step, 0)

    def expand(j, s_buf, du_buf):
        rows = pl.ds(pl.multiple_of(j * SUB, SUB), SUB)
        yj = y_s[:, rows, :].reshape(144, BLK)
        dzj = dm_s[1:, rows, :].reshape(CH, BLK)
        for r0 in range(0, GRID_ROWS, CHUNK):
            half = mm(kg[r0:r0 + CHUNK, 0:144], yj).astype(BF16).astype(F32)
            dval = mm(kf[r0:r0 + CHUNK, :], dzj).astype(BF16).astype(F32)
            th = jnp.tanh(half)
            plus = 1.0 + th
            val = half * plus
            s_buf[r0:r0 + CHUNK, :] = val.astype(BF16)
            du_buf[r0:r0 + CHUNK, :] = (dval * (plus + val * (1.0 - th))).astype(BF16)

    def contract(j, s_buf, du_buf):
        rows = pl.ds(pl.multiple_of(j * SUB, SUB), SUB)
        m_s[1:, rows, :] = mm(kft[...], s_buf[...]).astype(BF16).reshape(8, SUB, BLK)
        dy_s[:, rows, :] = mm(kgt[...], du_buf[...]).astype(BF16).reshape(9, SUB, BLK)

    expand(0, s_bufs[0], du_bufs[0])

    def grid_step(i, carry):
        expand(2 * i + 1, s_bufs[1], du_bufs[1])
        contract(2 * i, s_bufs[0], du_bufs[0])
        expand(jnp.minimum(2 * i + 2, 31), s_bufs[0], du_bufs[0])
        contract(2 * i + 1, s_bufs[1], du_bufs[1])
        return carry
    lax.fori_loop(0, 16, grid_step, 0)

    def down_step(coef, carry):
        degree = degree_of(coef)
        mk = m_s[coef]
        dyk = dy_s[coef]
        gk = g_ref[coef, :, lanes]
        nk = n_s[coef]
        xk = x_ref[coef, :, lanes].astype(F32)
        out_ref[coef, :, lanes] = (xk + mm(wdown_t[degree], mk)).astype(BF16)
        dn_s[coef] = mm(wup[degree], dyk)
        base = pl.multiple_of(degree * CH, CH)
        g_up = mm_nt(nk, dyk)
        for t in range(TP):
            grad_ref[t, pl.ds(base, CH), :] += g_up[:, t * CH:(t + 1) * CH]
            grad_ref[t, pl.ds(base + HID, CH), :] += mm_nt(mk[t * CH:(t + 1) * CH, :], gk)
        return carry
    lax.fori_loop(0, COEFS, down_step, 0)
    dn_s[0] += mm(wgate[...], da_s[...])
    g_gate = mm_nt(n_s[0], da_s[...])
    for t in range(TP):
        grad_ref[t, 384:HID, :] += g_gate[:, t * CH:(t + 1) * CH]

    x0 = x_ref[0, :, lanes].astype(F32)
    hat = (x0 - mean_s) * inv_s
    dh = dn_s[0].astype(BF16).astype(F32) * gain[0]
    m1 = jnp.sum(dh, axis=0, keepdims=True) * (1.0 / CH)
    m2 = jnp.sum(dh * hat, axis=0, keepdims=True) * (1.0 / CH)
    dx_ref[0, :, lanes] = (inv_s * (dh - m1 - hat * m2) + g_ref[0, :, lanes].astype(F32)).astype(BF16)
    acc = jnp.zeros((CH, BLK), F32)
    for coef in range(1, COEFS):
        xk = x_ref[coef, :, lanes].astype(F32)
        acc = acc + (dn_s[coef].astype(BF16).astype(F32) * gain[1 if coef < 4 else 2]) * (xk * inv_v)
    mv = jnp.sum(acc, axis=0, keepdims=True) * (1.0 / 1024)
    for coef in range(1, COEFS):
        xk = x_ref[coef, :, lanes].astype(F32)
        dh = dn_s[coef].astype(BF16).astype(F32) * gain[1 if coef < 4 else 2]
        dx_ref[coef, :, lanes] = (inv_v * (dh - (xk * inv_v) * mv) + g_ref[coef, :, lanes].astype(F32)).astype(BF16)


CHUNK = 144


def compute_kernel(x_ref, g_ref, gain_ref, wup, wgate, wdown, tog_ref, frg_ref, out_ref, dx_ref, grad_ref,
                   wup_t, wgate_t, wdown_t, kg, kf, kft, kgt, n_s, y_s, dm_s, m_s, dy_s, da_s, dn_s, sb0, sb1, db0, db1):
    setup_tables(tog_ref, frg_ref, kg, kf, kft, kgt)
    for degree in range(DEGS):
        wup_t[degree] = wup[degree].T
        wdown_t[degree] = wdown[degree].T
    wgate_t[...] = wgate[...].T
    for buf in (sb0, sb1, db0, db1):
        buf[GRID_ROWS:GRID_PAD, :] = jnp.zeros((64, BLK), BF16)
    grad_ref[...] = jnp.zeros(grad_ref.shape, F32)

    def block_step(b, carry):
        lanes = pl.ds(pl.multiple_of(b * BLK, BLK), BLK)
        compute_block(lanes, x_ref, g_ref, gain_ref, wup, wgate, wdown, out_ref, dx_ref, grad_ref,
                      wup_t, wgate_t, wdown_t, kg, kf, kft, kgt, n_s, y_s, dm_s, m_s, dy_s, da_s, dn_s, (sb0, sb1), (db0, db1))
        return carry
    lax.fori_loop(0, x_ref.shape[2] // BLK, block_step, 0)


def scratch_list():
    v = pltpu.VMEM
    return [v((DEGS, HID, CH), BF16), v((HID, CH), BF16), v((DEGS, CH, HID), BF16),
            v((GRID_ROWS, BLK), BF16), v((GRID_ROWS, CH), BF16), v((CH, GRID_PAD), BF16), v((144, GRID_PAD), BF16),
            v((COEFS, CH, BLK), BF16), v((COEFS, HID, BLK), BF16), v((COEFS, HID, BLK), BF16), v((COEFS, HID, BLK), BF16),
            v((COEFS, HID, BLK), BF16), v((HID, BLK), BF16), v((COEFS, CH, BLK), F32),
            v((GRID_PAD, BLK), BF16), v((GRID_PAD, BLK), BF16), v((GRID_PAD, BLK), BF16), v((GRID_PAD, BLK), BF16)]


def compute_call(x, g, gain, wup, wgate, wdown, tog, frg):
    vm = pl.BlockSpec(memory_space=pltpu.VMEM)
    return pl.pallas_call(
        compute_kernel,
        out_shape=[jax.ShapeDtypeStruct(x.shape, BF16), jax.ShapeDtypeStruct(x.shape, BF16), jax.ShapeDtypeStruct((4, ROWS, CH), F32)],
        in_specs=[vm] * 8, out_specs=[vm] * 3, scratch_shapes=scratch_list(),
        compiler_params=pltpu.CompilerParams(vmem_limit_bytes=VMEM_LIMIT), name="ffn",
    )(x, g, gain, wup, wgate, wdown, tog, frg)


MESH = pl.DeviceIdType.MESH


def places():
    dp = lax.axis_index("dp")
    return lax.axis_index("tp"), dp // 8, (dp // 2) % 4, dp % 2


def dp_index(z, y, core):
    return (z * 4 + y) * 2 + core


def meet(peers):
    barrier = pltpu.get_barrier_semaphore()
    for peer in peers:
        pl.semaphore_signal(barrier, inc=1, device_id=peer, device_id_type=MESH)
    pl.semaphore_wait(barrier, len(peers))


def remote(src, dst, send_sem, recv_sem, peer):
    return pltpu.make_async_remote_copy(src_ref=src, dst_ref=dst, send_sem=send_sem, recv_sem=recv_sem,
                                        device_id=peer, device_id_type=MESH)


def part(i, size):
    return pl.ds(pl.multiple_of(i * size, size), size)


def gather_kernel(x_loc, g_loc, gain_loc, up_loc, gate_loc, down_loc, x_all, g_all, gain_all, up_all, gate_all, down_all,
                  act_send, act_recv, w_send, w_recv, pair_send, pair_recv, loc_sem):
    me, z, y, core = places()
    atoms = x_all.shape[2]
    pair = {"dp": dp_index(z, y, 1 - core)}
    meet([{"tp": lax.rem(me + d, TP)} for d in range(1, TP)] + [pair])
    half = part(core, 64)
    mine = part(me, CH)

    pieces = [
        (up_loc.at[:, half, :], up_all.at[:, half, mine]),
        (gate_loc.at[half, :], gate_all.at[half, mine]),
        (down_loc.at[:, half, :], down_all.at[:, part(2 * me + core, 64), :]),
    ]
    copies = []
    for d in range(1, TP):
        peer = {"tp": lax.rem(me + d, TP)}
        for i, (src, dst) in enumerate(pieces):
            copies.append(remote(src, dst, w_send.at[d - 1, i], w_recv.at[d - 1, i], peer))
        copies.append(remote(gain_loc, gain_all.at[:, part(me, 32), :], w_send.at[d - 1, 3], w_recv.at[d - 1, 3], peer))
    acts = []
    for d in range(1, TP):
        tgt = lax.rem(me + d, TP)
        peer = {"tp": tgt}
        for i, (src, dst) in enumerate(((x_loc, x_all), (g_loc, g_all))):
            acts.append(remote(src.at[:, :, part(tgt, atoms)], dst.at[:, part(me, 32), :], act_send.at[d - 1, i], act_recv.at[d - 1, i], peer))
    for c in copies + acts:
        c.start()
    local = [pltpu.make_async_copy(src, dst, loc_sem.at[i]) for i, (src, dst) in enumerate(
        pieces + [(gain_loc, gain_all.at[:, part(me, 32), :]), (x_loc.at[:, :, part(me, atoms)], x_all.at[:, part(me, 32), :]),
                  (g_loc.at[:, :, part(me, atoms)], g_all.at[:, part(me, 32), :])])]
    for c in local:
        c.start()
    for c in local:
        c.wait()
    for c in copies:
        c.wait_recv()
    pairs = [remote(up_all.at[:, half, :], up_all.at[:, half, :], pair_send.at[0], pair_recv.at[0], pair),
             remote(gate_all.at[half, :], gate_all.at[half, :], pair_send.at[1], pair_recv.at[1], pair)]
    for t in range(TP):
        rows = pl.ds(pl.multiple_of(t * CH + core * 64, 64), 64)
        pairs.append(remote(down_all.at[:, rows, :], down_all.at[:, rows, :], pair_send.at[2 + t], pair_recv.at[2 + t], pair))
    for c in pairs:
        c.start()
    for c in pairs:
        c.wait_recv()
    for c in acts:
        c.wait_recv()
    for c in copies + acts + pairs:
        c.wait_send()


def gather_call(x, g, gain, up, gate, down):
    vm = pl.BlockSpec(memory_space=pltpu.VMEM)
    hbm = pl.BlockSpec(memory_space=pl.ANY)
    dma = pltpu.SemaphoreType.DMA
    atoms = x.shape[2] // 4
    sds = jax.ShapeDtypeStruct
    return pl.pallas_call(
        gather_kernel,
        out_shape=[sds((COEFS, CH, atoms), BF16), sds((COEFS, CH, atoms), BF16), sds((DEGS, CH, CH), F32),
                   sds((DEGS, CH, HID), BF16), sds((CH, HID), BF16), sds((DEGS, HID, CH), BF16)],
        in_specs=[hbm] * 2 + [vm] * 4, out_specs=[vm] * 6,
        scratch_shapes=[dma((DEGS, 2)), dma((DEGS, 2)), dma((DEGS, 4)), dma((DEGS, 4)), dma((6,)), dma((6,)), dma((6,))],
        compiler_params=pltpu.CompilerParams(collective_id=0, has_side_effects=True, vmem_limit_bytes=VMEM_LIMIT), name="gather",
    )(x, g, gain, up, gate, down)


def scatter_kernel(out_all, dx_all, wg, out_loc, dx_loc, d_up, d_gate, d_down,
                   r1, a1, r2, a2, r3, a3, r4, fin, r5, r7, full,
                   act_send, act_recv, loc_sem, s1, q1, s2, q2, s3, q3, s4, q4, s5, q5, s6, q6):
    me, z, y, core = places()
    atoms = out_all.shape[2]
    pair = {"dp": dp_index(z, y, 1 - core)}
    x_peers = [{"tp": lax.rem(me + d, TP)} for d in range(1, TP)]
    z_peers = [{"dp": dp_index(lax.rem(z + d, 8), y, core)} for d in range(1, 8)]
    group = [(dy, dc) for dc in range(2) for dy in range(TP) if (dy, dc) != (0, 0)]
    yc_peers = [{"dp": dp_index(z, lax.rem(y + dy, 4), lax.rem(core + dc, 2))} for dy, dc in group]
    meet(x_peers + z_peers + yc_peers)
    sent = []
    c1 = remote(wg.at[:, part(1 - core, 8)], r1, s1, q1, pair)
    c1.start()
    sent.append(c1)
    acts = []
    for d in range(1, TP):
        tgt = lax.rem(me + d, TP)
        for i, (src, dst) in enumerate(((out_all, out_loc), (dx_all, dx_loc))):
            acts.append(remote(src.at[:, part(tgt, 32), :], dst.at[:, :, part(me, atoms)], act_send.at[d - 1, i], act_recv.at[d - 1, i], {"tp": tgt}))
    local = [pltpu.make_async_copy(src.at[:, part(me, 32), :], dst.at[:, :, part(me, atoms)], loc_sem.at[i])
             for i, (src, dst) in enumerate(((out_all, out_loc), (dx_all, dx_loc)))]
    for c in acts + local:
        c.start()
    c1.wait_recv()

    def sum1(i, carry):
        t, s = i // 8, i % 8
        a1[t, s] = wg[t, core * 8 + s] + r1[t, s]
        return carry
    lax.fori_loop(0, 32, sum1, 0)
    c2 = []
    for d in range(1, TP):
        ty = lax.rem(y + d, TP)
        c2.append(remote(a1.at[:, part(ty, 2)], r2.at[d - 1], s2.at[d - 1], q2.at[d - 1], {"dp": dp_index(z, ty, core)}))
    for c in c2:
        c.start()
    for c in c2:
        c.wait_recv()

    def sum2(i, carry):
        t, s = i // 2, i % 2
        a2[i] = (a1[t, y * 2 + s] + r2[0, t, s]) + (r2[1, t, s] + r2[2, t, s])
        return carry
    lax.fori_loop(0, 8, sum2, 0)
    c3 = []
    for d in range(1, 8):
        tz = lax.rem(z + d, 8)
        c3.append(remote(a2.at[tz], r3.at[d - 1], s3.at[d - 1], q3.at[d - 1], {"dp": dp_index(tz, y, core)}))
    for c in c3:
        c.start()
    for c in c3:
        c.wait_recv()
    a3[...] = ((a2[z] + r3[0]) + (r3[1] + r3[2])) + ((r3[3] + r3[4]) + (r3[5] + r3[6]))
    c4 = [remote(a3, r4.at[d - 1], s4.at[d - 1], q4.at[d - 1], x_peers[d - 1]) for d in range(1, TP)]
    for c in c4:
        c.start()
    for c in c4:
        c.wait_recv()
    half = lax.rem(z, 2)
    owner = me == z // 2
    fin[...] = ((a3[...] + r4[0]) + (r4[1] + r4[2])).astype(BF16)
    c5 = [remote(fin, r5.at[half], s5.at[d - 1], q5.at[half], z_peers[d - 1]) for d in range(1, 8)]

    @pl.when(owner)
    def _():
        for c in c5:
            c.start()
        r5[half] = fin[...]
    for h in range(2):
        @pl.when(z != 2 * me + h)
        def _():
            remote(fin, r5.at[h], s5.at[0], q5.at[h], z_peers[0]).wait_recv()
    slot = core * 4 + y
    c6 = [remote(r5, r7.at[slot], s6.at[i], q6.at[i], yc_peers[i]) for i in range(7)]
    for c in c6:
        c.start()
    r7[slot] = r5[...]
    for c in c6:
        c.wait_recv()
    for s in range(16):
        full[s * SLAB:(s + 1) * SLAB, :] = r7[s // 2, s % 2].astype(F32)
    for degree in range(DEGS):
        d_up[degree] = full[degree * CH:(degree + 1) * CH, :].astype(BF16)
        d_down[degree] = full[HID + degree * CH:GRID_PAD + degree * CH, :].astype(BF16)
    d_gate[...] = full[384:HID, :].astype(BF16)
    for c in acts:
        c.wait_recv()
    for c in local:
        c.wait()
    for c in acts + sent + c2 + c3 + c4 + c6:
        c.wait_send()

    @pl.when(owner)
    def _():
        for c in c5:
            c.wait_send()


def scatter_call(out, dx, wg):
    vm = pl.BlockSpec(memory_space=pltpu.VMEM)
    hbm = pl.BlockSpec(memory_space=pl.ANY)
    dma = pltpu.SemaphoreType.DMA
    v = pltpu.VMEM
    sds = jax.ShapeDtypeStruct
    atoms = out.shape[2]
    return pl.pallas_call(
        scatter_kernel,
        out_shape=[sds((COEFS, 32, atoms * 4), BF16), sds((COEFS, 32, atoms * 4), BF16), sds((DEGS, CH, CH), BF16), sds((CH, CH), BF16), sds((DEGS, CH, CH), BF16)],
        in_specs=[vm] * 3, out_specs=[hbm] * 2 + [vm] * 3,
        scratch_shapes=[v((TP, 8, SLAB, CH), F32), v((TP, 8, SLAB, CH), F32), v((DEGS, 4, 2, SLAB, CH), F32), v((8, SLAB, CH), F32),
                        v((7, SLAB, CH), F32), v((SLAB, CH), F32), v((DEGS, SLAB, CH), F32), v((SLAB, CH), BF16), v((2, SLAB, CH), BF16),
                        v((8, 2, SLAB, CH), BF16), v((ROWS, CH), F32),
                        dma((DEGS, 2)), dma((DEGS, 2)), dma((2,)), dma, dma, dma((3,)), dma((3,)), dma((7,)), dma((7,)), dma((3,)), dma((3,)),
                        dma((7,)), dma((2,)), dma((7,)), dma((7,))],
        compiler_params=pltpu.CompilerParams(collective_id=1, has_side_effects=True, vmem_limit_bytes=VMEM_LIMIT), name="scatter",
    )(out, dx, wg.reshape(4, 16, SLAB, CH))


def solution(mesh):
    act = P('dp', None, 'tp')
    in_specs = (act, P(None, 'tp'), P(None, None, 'tp'), P(None, 'tp'), P(None, 'tp', None), P(None, None), P(None, None), act)
    out_specs = (act, act, P(None, None, 'tp'), P(None, 'tp'), P(None, 'tp', None))

    def local_step(x, gain, up, gate, down, tog, frg, g):
        gain_b = jnp.broadcast_to(gain[:, :, None], (3, 32, CH))
        tog_p = jnp.pad(tog, ((0, 119), (0, 92)))
        frg_p = jnp.pad(frg, ((0, 92), (0, 120)))
        x_all, g_all, gain_all, up_all, gate_all, down_all = gather_call(x.transpose(1, 2, 0), g.transpose(1, 2, 0), gain_b, up, gate, down)
        out_all, dx_all, wg = compute_call(x_all, g_all, gain_all, up_all, gate_all, down_all, tog_p, frg_p)
        out, dx, d_up, d_gate, d_down = scatter_call(out_all, dx_all, wg)
        return out.transpose(2, 0, 1), dx.transpose(2, 0, 1), d_up, d_gate, d_down

    return jax.shard_map(local_step, mesh=mesh, in_specs=in_specs, out_specs=out_specs, check_vma=False)
```

time: 825 us -> 145 us (0.18)
  the two profiles are of different devices: /device:TPU:4 before, /device:TPU:3 now
where the time goes in v1:
time: 145 us; the launch traced here: 144 us
  Pallas kernels  133 us (92%)
  local copies, waits for them, and re-layouts  9.55 us (7%)
    pallas_call x1, Pallas kernels, scatter_call(): pl.pallas_call(scatter_kernel, out_shape=[sds((COEFS, 32, atoms * 4), BF1...  50.5 us
    pallas_call x1, Pallas kernels, compute_call(): pl.pallas_call(compute_kernel, out_shape=[jax.ShapeDtypeStruct(x.shape, B...  44.9 us
    pallas_call x1, Pallas kernels, gather_call(): pl.pallas_call(gather_kernel, out_shape=[sds((COEFS, CH, atoms), BF16), s...  38.1 us
    unnamed x14, local copies, waits for them, and re-layouts  6.21 us

profile of v1, /device:TPU:3, one launch (start us, length us, event | category | flops | bytes accessed | tf_op | source)
XLA Modules:
  0.0 143.7 jit_solution(8747523282734726099)
XLA Ops:
  0.6 0.8 copy.13
  1.4 0.6 pad.9.frg_ref
  2.0 1.4 broadcast_in_dim.2.gain_loc
  3.4 1.3 pad.8.tog_ref
  4.8 38.1 %gather.1 = (bf16[9,128,512]{2,1,0:T(8,128)(2,1)}, bf16[9,128,512]{2,1,0:T(8,128)(2,1)}, f32[3,128,128]{2,1,0:T(8,128)}, bf16[3,128,512]{2,1,0:T(8,128)(2,1)}, b...) custom-call(bf16[9,32,2048]{2,1,0:T(8,128)(2,1)} %bitcast.6, bf16[9,32,2048]{2,1,0:T(8,128)(2,1)} %bitcast.7, ...), custom_call_target="tpu_custom_call" | custom-call | tf_op jit(solution)/shard_map/gather/pallas_call | solution.py:293
  42.9 44.9 %ffn.1 = (bf16[9,128,512]{2,1,0:T(8,128)(2,1)}, bf16[9,128,512]{2,1,0:T(8,128)(2,1)}, f32[4,896,128]{2,1,0:T(8,128)}) custom-call(bf16[9,128,512]{2,1,0:T(8,128)(2,1)} %get-tuple-element.19.x_ref, bf16[9,128,512]{2,1,0:T(8,128)(2,1)} %get-tuple-element.20.g_ref, f32[3,128,128]{2,1,0:T(8,128)} %get-tuple-element.21.gain_ref, ...), custom_call_target="tpu_custom_call" | custom-call | tf_op jit(solution)/shard_map/ffn/pallas_call | solution.py:199
  87.8 50.5 %scatter.1 = (bf16[9,32,2048]{2,1,0:T(8,128)(2,1)}, bf16[9,32,2048]{2,1,0:T(8,128)(2,1)}, bf16[3,128,128]{2,1,0:T(8,128)(2,1)}, bf16[128,128]{1,0:T(8,128)(2,1)}, bf16[3,128,128]{2,1,0:T(8,128)(2,1)}) custom-call(bf16[9,128,512]{2,1,0:T(8,128)(2,1)} %get-tuple-element.25.out_all, bf16[9,128,512]{2,1,0:T(8,128)(2,1)} %get-tuple-element.26.dx_all, ...), custom_call_target="tpu_custom_call" | custom-call | tf_op jit(solution)/shard_map/scatter/pallas_call | solution.py:409
  138.2 0.0 copy-start
  138.2 2.5 %copy.19 = bf16[2048,9,32]{0,2,1:T(8,128)(2,1)} copy(bf16[2048,9,32]{0,2,1:T(8,128)(2,1)} %bitcast.9) | data formatting | bytes 2359296
  140.7 0.0 copy-done
  140.7 0.0 copy-start.2
  140.7 0.0 copy-start.3
  140.7 0.0 copy-start.1
  140.8 1.0 copy.20
  141.8 0.0 copy-done.2
  141.8 0.6 copy.21
  142.4 0.0 copy-done.3
  142.4 0.6 copy.22
  143.0 0.0 copy-done.1
  143.0 0.6 copy.23
Async XLA Ops:
  138.2 2.5 %copy-start = (bf16[9,32,2048]{2,1,0:T(8,128)(2,1)S(1)}, bf16[9,32,2048]{2,1,0:T(8,128)(2,1)}, u32[]{:S(2)}) copy-start(bf16[9,32,2048]{2,1,0:T(8,128)(2,1)} %get-tuple-element.29) | copy-start | bytes 3538948
  140.7 1.0 copy-start.2
  140.7 1.7 %copy-start.3 = (bf16[128,128]{1,0:T(8,128)(2,1)S(1)}, bf16[128,128]{1,0:T(8,128)(2,1)}, u32[]{:S(2)}) copy-start(bf16[128,128]{1,0:T(8,128)(2,1)} %get-tuple-element.41) | copy-start | bytes 98308
  140.7 2.3 %copy-start.1 = (bf16[3,128,128]{2,1,0:T(8,128)(2,1)S(1)}, bf16[3,128,128]{2,1,0:T(8,128)(2,1)}, u32[]{:S(2)}) copy-start(bf16[3,128,128]{2,1,0:T(8,128)(2,1)} %get-tuple-element.42) | copy-start | bytes 294916

commit v2 on v0

v2 whole, which is shorter than its diff:
```python
import functools
import jax
import jax.numpy as jnp
from jax import lax
from jax.experimental import pallas as pl
from jax.experimental.pallas import tpu as pltpu
from jax.sharding import PartitionSpec as P

NORM_EPS = 1e-5
COEFS = 9
CH = 128
HID = 512
SUB = 16
BLK = 256
GRID_ROWS = 576
GRID_PAD = 640
SLAB = 56
ROWS = 896
TILE = 16
EIGHTH = 112
NZ = 8
DEGS = 3
TP = 4
SLICE = 32
PTS = 36
VEC_SCALE = 1.0 / 1024
VMEM_LIMIT = 60 * 2**20
F32 = jnp.float32
BF16 = jnp.bfloat16


def iota(shape, axis):
    return lax.broadcasted_iota(jnp.int32, shape, axis)


def mm(a, b):
    return jnp.dot(a, b, preferred_element_type=F32)


def mm_nt(a, b):
    return lax.dot_general(a, b, (((1,), (1,)), ((), ())), preferred_element_type=F32)


def one_hot(shape, row_div, col_div):
    return jnp.where(iota(shape, 0) // row_div == iota(shape, 1) // col_div, 1.0, 0.0).astype(BF16)


def spread(table, rows, row_div, cols, col_div):
    left = mm(one_hot((rows, CH), row_div, 1), table).astype(BF16)
    full = mm(left, one_hot((CH, cols), 1, col_div))
    same = iota((rows, cols), 0) % SUB == iota((rows, cols), 1) % SUB
    return jnp.where(same, full, 0.0)


def degree_of(coef):
    return jnp.where(coef >= 4, 2, jnp.where(coef >= 1, 1, 0))


MESH = pl.DeviceIdType.MESH


def places():
    dp = lax.axis_index("dp")
    return lax.axis_index("tp"), dp // NZ, (dp // 2) % TP, dp % 2


def dp_index(z, y, core):
    return (z * TP + y) * 2 + core


def remote(src, dst, send_sem, recv_sem, peer):
    return pltpu.make_async_remote_copy(src_ref=src, dst_ref=dst, send_sem=send_sem, recv_sem=recv_sem,
                                        device_id=peer, device_id_type=MESH)


def part(i, size):
    return pl.ds(pl.multiple_of(i * size, size), size)


def start(copies):
    for c in copies:
        c.start()


def arrive(copies):
    for c in copies:
        c.wait_recv()


CHUNK = 144
GROUPS = HID // SUB
BLOCKS = 2


def step_kernel(x_loc, g_loc, gain_loc, up_loc, gate_loc, down_loc, tog_ref, frg_ref,
                out_loc, dx_loc, d_up, d_gate, d_down,
                x_all, g_all, gain_x, up_all, gate_all, down_all, out_all, dx_all, wg, pad_s, gain_b,
                wup_t, wgate_t, wdown_t, kg, kf, kft, kgt, n_s, y_s, dm_s, m_s, dy_s, da_s, dn_s, sb0, sb1, db0, db1,
                r1, a1, r2, a2, r3, a3, r4, fin, r5, r7,
                act_send, act_recv, wx_send, wx_recv, wy_send, wy_recv, wc_send, wc_recv, gain_send, gain_recv, loc_sem,
                o_send, o_recv, oloc_sem, s1, q1, s2, q2, s3, q3, s4, q4, s5, q5, s6, q6):
    me, z, y, core = places()
    atoms = x_all.shape[2]
    pair = {"dp": dp_index(z, y, 1 - core)}
    x_dist = list(range(1, TP))
    x_peers = [{"tp": lax.rem(me + d, TP)} for d in x_dist]
    y_peers = [{"dp": dp_index(z, lax.rem(y + d, TP), core)} for d in x_dist]
    z_peers = [{"dp": dp_index(lax.rem(z + d, NZ), y, core)} for d in range(1, NZ)]
    group = [(dy, dc) for dc in range(2) for dy in range(TP) if dy + dc > 0]
    yc_peers = [{"dp": dp_index(z, lax.rem(y + dy, TP), lax.rem(core + dc, 2))} for dy, dc in group]
    barrier = pltpu.get_barrier_semaphore()
    meeting = x_peers + z_peers + yc_peers
    for peer in meeting:
        pl.semaphore_signal(barrier, inc=1, device_id=peer, device_id_type=MESH)
    pl.semaphore_wait(barrier, len(meeting))

    eighth = part(core * TP + y, TILE)
    mine = part(me, CH)
    pieces = [(up_loc.at[:, eighth, :], up_all.at[:, eighth, mine]),
              (gate_loc.at[eighth, :], gate_all.at[eighth, mine]),
              (down_loc.at[:, eighth, :], down_all.at[:, me, eighth, :])]
    wx = [remote(src, dst, wx_send.at[d, i], wx_recv.at[d, i], peer)
          for d, peer in enumerate(x_peers) for i, (src, dst) in enumerate(pieces)]
    gx = [remote(gain_loc, gain_x.at[me], gain_send.at[d], gain_recv.at[d], peer) for d, peer in enumerate(x_peers)]
    start(wx + gx)
    acts = []
    for b in range(BLOCKS):
        acts.append([])
        for d, peer in enumerate(x_peers):
            tgt = lax.rem(me + d + 1, TP)
            cols = part(tgt * BLOCKS + b, BLK)
            for i, (src, dst) in enumerate(((x_loc, x_all), (g_loc, g_all))):
                acts[b].append(remote(src.at[:, :, cols], dst.at[:, part(me, SLICE), part(b, BLK)], act_send.at[b, d, i], act_recv.at[b, d, i], peer))
        start(acts[b])
    local = [pltpu.make_async_copy(src, dst, loc_sem.at[i]) for i, (src, dst) in enumerate(
        pieces + [(x_loc.at[:, :, part(me, atoms)], x_all.at[:, part(me, SLICE), :]), (g_loc.at[:, :, part(me, atoms)], g_all.at[:, part(me, SLICE), :])])]
    start(local)

    pad_s[...] = jnp.zeros(pad_s.shape, F32)
    pad_s[0, 0:COEFS, 0:PTS] = tog_ref[...]
    pad_s[1, 0:COEFS - 1, 0:PTS] = frg_ref[...]
    tog, tog_t = pad_s[0].astype(BF16), pad_s[0].T.astype(BF16)
    frg_t, frg = pad_s[1].astype(BF16), pad_s[1].T.astype(BF16)
    kg[...] = (0.5 * spread(tog_t, GRID_ROWS, SUB, BLK, SUB)).astype(BF16)
    kf[...] = (0.5 * spread(frg, GRID_ROWS, SUB, CH, SUB)).astype(BF16)
    kft[...] = spread(frg_t, CH, SUB, GRID_PAD, SUB).astype(BF16)
    kgt[...] = spread(tog, CHUNK, SUB, GRID_PAD, SUB).astype(BF16)
    for buf in (sb0, sb1, db0, db1):
        buf[GRID_ROWS:GRID_PAD, :] = jnp.zeros((GRID_PAD - GRID_ROWS, BLK), BF16)
    wg[...] = jnp.zeros(wg.shape, F32)
    gain_x[me] = gain_loc[...]
    for c in local:
        c.wait()
    arrive(wx)
    wholes = [lambda rows: up_all.at[:, rows, :], lambda rows: gate_all.at[rows, :], lambda rows: down_all.at[:, :, rows, :]]
    wy = [remote(whole(eighth), whole(eighth), wy_send.at[d, i], wy_recv.at[d, i], peer)
          for d, peer in enumerate(y_peers) for i, whole in enumerate(wholes)]
    start(wy)
    arrive(gx)
    for t in range(TP):
        pad_s[2, t * NZ:t * NZ + DEGS, 0:SLICE] = gain_x[t]
    cols = pad_s[2].T
    for t in range(TP):
        for degree in range(DEGS):
            col = t * NZ + degree
            gain_b[degree, t * SLICE:(t + 1) * SLICE, :] = jnp.broadcast_to(cols[0:SLICE, col:col + 1], (SLICE, BLK))
    arrive(wy)
    side = part(core, CH // 2)
    wc = [remote(whole(side), whole(side), wc_send.at[i], wc_recv.at[i], pair) for i, whole in enumerate(wholes)]
    start(wc)
    arrive(wc)
    for degree in range(DEGS):
        wup_t[degree] = up_all[degree].T
        wdown_t[degree] = down_all[degree].reshape(HID, CH).T
    wgate_t[...] = gate_all[...].T

    def gain_of(coef):
        return gain_b[0 if coef == 0 else (1 if coef < TP else 2)]

    def norm(lanes):
        x0 = x_all[0, :, lanes].astype(F32)
        mean_s = jnp.sum(x0, axis=0, keepdims=True) * (1.0 / CH)
        cen = x0 - mean_s
        inv_s = lax.rsqrt(jnp.sum(cen * cen, axis=0, keepdims=True) * (1.0 / CH) + NORM_EPS)
        n_s[0] = ((cen * inv_s) * gain_of(0)).astype(BF16)
        acc = jnp.zeros((CH, BLK), F32)
        for coef in range(1, COEFS):
            xk = x_all[coef, :, lanes].astype(F32)
            acc = acc + xk * xk
        inv_v = lax.rsqrt(jnp.sum(acc, axis=0, keepdims=True) * VEC_SCALE + NORM_EPS)
        for coef in range(1, COEFS):
            xk = x_all[coef, :, lanes].astype(F32)
            n_s[coef] = ((xk * inv_v) * gain_of(coef)).astype(BF16)
        return mean_s, inv_s, inv_v

    def up(lanes):
        def up_step(coef, carry):
            degree = degree_of(coef)
            y_s[coef] = mm(wup_t[degree], n_s[coef]).astype(BF16)
            dm_s[coef] = mm(down_all[degree].reshape(HID, CH), g_all[coef, :, lanes]).astype(BF16)
            return carry
        lax.fori_loop(0, COEFS, up_step, 0)

        def gate_step(i, carry):
            rows = part(i, CH)
            half = (0.5 * mm(wgate_t[rows, :], n_s[0])).astype(BF16).astype(F32)
            th = jnp.tanh(half)
            plus = 1.0 + th
            val = half * plus
            m_s[0, rows, :] = val.astype(BF16)
            slope = 0.5 * (plus + val * (1.0 - th))
            da_s[rows, :] = (dm_s[0, rows, :].astype(F32) * slope).astype(BF16)
            return carry
        lax.fori_loop(0, TP, gate_step, 0)

    def expand(j, s_buf, du_buf):
        rows = part(j, SUB)
        yj = y_s[:, rows, :].reshape(CHUNK, BLK)
        dzj = dm_s[1:, rows, :].reshape(CH, BLK)
        for r0 in range(0, GRID_ROWS, CHUNK):
            half = mm(kg[r0:r0 + CHUNK, 0:CHUNK], yj).astype(BF16).astype(F32)
            dval = mm(kf[r0:r0 + CHUNK, :], dzj).astype(BF16).astype(F32)
            th = jnp.tanh(half)
            plus = 1.0 + th
            val = half * plus
            s_buf[r0:r0 + CHUNK, :] = val.astype(BF16)
            du_buf[r0:r0 + CHUNK, :] = (dval * (plus + val * (1.0 - th))).astype(BF16)

    def contract(j, s_buf, du_buf):
        rows = part(j, SUB)
        m_s[1:, rows, :] = mm(kft[...], s_buf[...]).astype(BF16).reshape(COEFS - 1, SUB, BLK)
        dy_s[:, rows, :] = mm(kgt[...], du_buf[...]).astype(BF16).reshape(COEFS, SUB, BLK)

    def grid_step(i, carry):
        expand(2 * i + 1, sb1, db1)
        contract(2 * i, sb0, db0)
        expand(jnp.minimum(2 * i + 2, GROUPS - 1), sb0, db0)
        contract(2 * i + 1, sb1, db1)
        return carry

    def weight_grads(t, lanes):
        rows = part(t, CH)

        def coef_step(coef, carry):
            base = degree_of(coef) * CH
            wg[t, part(degree_of(coef), CH), :] += mm_nt(n_s[coef], dy_s[coef, rows, :])
            wg[t, part(degree_of(coef) + TP, CH), :] += mm_nt(m_s[coef, rows, :], g_all[coef, :, lanes])
            return carry
        lax.fori_loop(0, COEFS, coef_step, 0)
        wg[t, part(DEGS, CH), :] += mm_nt(n_s[0], da_s[rows, :])

    def down(lanes):
        def down_step(coef, carry):
            degree = degree_of(coef)
            xk = x_all[coef, :, lanes].astype(F32)
            out_all[coef, :, lanes] = (xk + mm(wdown_t[degree], m_s[coef])).astype(BF16)
            dn_s[coef] = mm(up_all[degree], dy_s[coef])
            return carry
        lax.fori_loop(0, COEFS, down_step, 0)
        dn_s[0] += mm(gate_all[...], da_s[...])

    def norm_back(lanes, mean_s, inv_s, inv_v):
        hat = (x_all[0, :, lanes].astype(F32) - mean_s) * inv_s
        dh = dn_s[0].astype(BF16).astype(F32) * gain_of(0)
        m1 = jnp.sum(dh, axis=0, keepdims=True) * (1.0 / CH)
        m2 = jnp.sum(dh * hat, axis=0, keepdims=True) * (1.0 / CH)
        dx_all[0, :, lanes] = (inv_s * (dh - m1 - hat * m2) + g_all[0, :, lanes].astype(F32)).astype(BF16)
        acc = jnp.zeros((CH, BLK), F32)
        for coef in range(1, COEFS):
            xk = x_all[coef, :, lanes].astype(F32)
            acc = acc + (dn_s[coef].astype(BF16).astype(F32) * gain_of(coef)) * (xk * inv_v)
        mv = jnp.sum(acc, axis=0, keepdims=True) * VEC_SCALE
        for coef in range(1, COEFS):
            xk = x_all[coef, :, lanes].astype(F32)
            dh = dn_s[coef].astype(BF16).astype(F32) * gain_of(coef)
            dx_all[coef, :, lanes] = (inv_v * (dh - (xk * inv_v) * mv) + g_all[coef, :, lanes].astype(F32)).astype(BF16)

    outs = ((out_all, out_loc), (dx_all, dx_loc))

    def out_copies(b, i):
        src, dst = outs[i]
        cols = part(me * BLOCKS + b, BLK)
        return [remote(src.at[:, part(lax.rem(me + d, TP), SLICE), part(b, BLK)], dst.at[:, :, cols],
                       o_send.at[b, i, d - 1], o_recv.at[b, i, d - 1], x_peers[d - 1]) for d in x_dist]

    def out_local(b, i):
        src, dst = outs[i]
        return pltpu.make_async_copy(src.at[:, part(me, SLICE), part(b, BLK)], dst.at[:, :, part(me * BLOCKS + b, BLK)], oloc_sem.at[b, i])

    sent = [[out_copies(b, i) for i in range(2)] for b in range(BLOCKS)]
    kept = [[out_local(b, i) for i in range(2)] for b in range(BLOCKS)]

    def send_out(b, i):
        start(sent[b][i])
        kept[b][i].start()

    half_rows = ROWS // 2
    c1 = [remote(wg.at[t, part(1 - core, half_rows), :], r1.at[t], s1.at[t], q1.at[t], pair) for t in range(TP)]
    c2 = [[remote(a1.at[t, part(lax.rem(y + d, TP), EIGHTH), :], r2.at[t, d - 1], s2.at[t, d - 1], q2.at[t, d - 1], y_peers[d - 1]) for d in x_dist]
          for t in range(TP)]
    c3 = [[remote(a2.at[t, part(lax.rem(lax.rem(z + d, NZ), NZ - 1), TILE), :], r3.at[t, d - 1], s3.at[t, d - 1], q3.at[t, d - 1], z_peers[d - 1])
           for d in range(1, NZ)] for t in range(TP)]
    c4 = [[remote(a3.at[t], r4.at[t, d - 1], s4.at[t, d - 1], q4.at[t, d - 1], x_peers[d - 1]) for d in x_dist] for t in range(TP)]
    c5 = [remote(fin, r5.at[part(z, TILE), :], s5.at[d - 1], q5.at[d - 1], z_peers[d - 1]) for d in range(1, NZ)]

    def sum_core(t):
        arrive([c1[t]])
        a1[t] = wg[t, part(core, half_rows), :] + r1[t]
        start(c2[t])

    def sum_y(t):
        arrive(c2[t])
        a2[t] = (a1[t, part(y, EIGHTH), :] + r2[t, 0]) + (r2[t, 1] + r2[t, 2])
        start(c3[t])

    def sum_z(t):
        arrive(c3[t])
        own = a2[t, part(lax.rem(z, NZ - 1), TILE), :]
        a3[t] = ((own + r3[t, 0]) + (r3[t, 1] + r3[t, 2])) + ((r3[t, 3] + r3[t, 4]) + (r3[t, 5] + r3[t, 6]))
        start(c4[t])

    def sum_x(t):
        arrive(c4[t])

        @pl.when(me == t)
        def _():
            fin[...] = ((a3[t] + r4[t, 0]) + (r4[t, 1] + r4[t, 2])).astype(BF16)
            start(c5)
            r5[part(z, TILE), :] = fin[...]

    first, second = pl.ds(0, BLK), pl.ds(BLK, BLK)
    arrive(acts[0])
    stats = norm(first)
    up(first)
    expand(0, sb0, db0)
    lax.fori_loop(0, GROUPS // 2, grid_step, 0)
    down(first)
    send_out(0, 0)
    norm_back(first, *stats)
    send_out(0, 1)

    def grads_step(t, carry):
        weight_grads(t, first)
        return carry
    lax.fori_loop(0, TP, grads_step, 0)

    arrive(acts[1])
    stats = norm(second)
    up(second)
    expand(0, sb0, db0)
    per = GROUPS // 2 // TP
    for t in range(TP):
        lax.fori_loop(t * per, (t + 1) * per, grid_step, 0)
        if t > 0:
            sum_core(t - 1)
        if t == TP - 1:
            sum_y(0)
        weight_grads(t, second)
        start([c1[t]])
    down(second)
    send_out(1, 0)
    sum_core(TP - 1)
    sum_y(1)
    norm_back(second, *stats)
    sum_z(0)
    sum_y(2)
    sum_z(1)
    sum_x(0)
    sum_y(3)
    sum_z(2)
    sum_x(1)
    sum_z(3)
    send_out(1, 1)
    sum_x(2)
    sum_x(3)
    arrive(c5)
    slot = part(core * TP + y, EIGHTH)
    c6 = [remote(r5.at[0:EIGHTH, :], r7.at[slot, :], s6.at[i], q6.at[i], yc_peers[i]) for i in range(len(group))]
    start(c6)
    r7[slot, :] = r5[0:EIGHTH, :]
    arrive(c6)
    for degree in range(DEGS):
        d_up[degree] = r7[degree * CH:(degree + 1) * CH, :]
        d_down[degree] = r7[(TP + degree) * CH:(TP + degree + 1) * CH, :]
    d_gate[...] = r7[DEGS * CH:TP * CH, :]
    finished = wx + gx + wy + wc + c1 + c5 + c6
    for group_of in acts + c2 + c3 + c4:
        finished = finished + group_of
    for b in range(BLOCKS):
        for i in range(2):
            arrive(sent[b][i])
            kept[b][i].wait()
            finished = finished + sent[b][i]
    for c in finished:
        c.wait_send()


def step_call(x, g, gain, up, gate, down, tog, frg):
    vm = pl.BlockSpec(memory_space=pltpu.VMEM)
    hbm = pl.BlockSpec(memory_space=pl.ANY)
    dma = pltpu.SemaphoreType.DMA
    v = pltpu.VMEM
    sds = jax.ShapeDtypeStruct
    atoms = x.shape[2] // TP
    act = (COEFS, CH, atoms)
    hid = (COEFS, HID, BLK)
    peers = TP - 1
    zs = NZ - 1
    return pl.pallas_call(
        step_kernel,
        out_shape=[sds(x.shape, BF16), sds(x.shape, BF16), sds((DEGS, CH, CH), BF16), sds((CH, CH), BF16), sds((DEGS, CH, CH), BF16)],
        in_specs=[hbm] * 2 + [vm] * 6, out_specs=[hbm] * 2 + [vm] * 3,
        scratch_shapes=[
            v(act, BF16), v(act, BF16), v((TP, DEGS, SLICE), F32), v((DEGS, CH, HID), BF16), v((CH, HID), BF16), v((DEGS, TP, CH, CH), BF16),
            v(act, BF16), v(act, BF16), v((TP, ROWS, CH), F32), v((DEGS, CH, CH), F32), v((DEGS, CH, BLK), F32),
            v((DEGS, HID, CH), BF16), v((HID, CH), BF16), v((DEGS, CH, HID), BF16),
            v((GRID_ROWS, BLK), BF16), v((GRID_ROWS, CH), BF16), v((CH, GRID_PAD), BF16), v((CHUNK, GRID_PAD), BF16),
            v((COEFS, CH, BLK), BF16), v(hid, BF16), v(hid, BF16), v(hid, BF16), v(hid, BF16), v((HID, BLK), BF16), v((COEFS, CH, BLK), F32),
            v((GRID_PAD, BLK), BF16), v((GRID_PAD, BLK), BF16), v((GRID_PAD, BLK), BF16), v((GRID_PAD, BLK), BF16),
            v((TP, ROWS // 2, CH), F32), v((TP, ROWS // 2, CH), F32), v((TP, peers, EIGHTH, CH), F32), v((TP, EIGHTH, CH), F32),
            v((TP, zs, TILE, CH), F32), v((TP, TILE, CH), F32), v((TP, peers, TILE, CH), F32), v((TILE, CH), BF16),
            v((NZ * TILE, CH), BF16), v((ROWS, CH), BF16),
            dma((BLOCKS, peers, 2)), dma((BLOCKS, peers, 2)), dma((peers, 3)), dma((peers, 3)), dma((peers, 3)), dma((peers, 3)), dma((3,)), dma((3,)),
            dma((peers,)), dma((peers,)), dma((5,)),
            dma((BLOCKS, 2, peers)), dma((BLOCKS, 2, peers)), dma((BLOCKS, 2)),
            dma((TP,)), dma((TP,)), dma((TP, peers)), dma((TP, peers)), dma((TP, zs)), dma((TP, zs)), dma((TP, peers)), dma((TP, peers)),
            dma((zs,)), dma((zs,)), dma((zs,)), dma((zs,))],
        compiler_params=pltpu.CompilerParams(collective_id=0, has_side_effects=True, vmem_limit_bytes=VMEM_LIMIT), name="step",
    )(x, g, gain, up, gate, down, tog, frg)


def solution(mesh):
    act = P('dp', None, 'tp')
    in_specs = (act, P(None, 'tp'), P(None, None, 'tp'), P(None, 'tp'), P(None, 'tp', None), P(None, None), P(None, None), act)
    out_specs = (act, act, P(None, None, 'tp'), P(None, 'tp'), P(None, 'tp', None))

    def local_step(x, gain, up, gate, down, tog, frg, g):
        out, dx, d_up, d_gate, d_down = step_call(x.transpose(1, 2, 0), g.transpose(1, 2, 0), gain, up, gate, down, tog, frg.T)
        return out.transpose(2, 0, 1), dx.transpose(2, 0, 1), d_up, d_gate, d_down

    return jax.shard_map(local_step, mesh=mesh, in_specs=in_specs, out_specs=out_specs, check_vma=False)
```

time: 825 us -> 116 us (0.14)
  the two profiles are of different devices: /device:TPU:4 before, /device:TPU:7 now
where the time goes in v2:
time: 116 us
  Pallas kernels  110 us (95%)
  local copies, waits for them, and re-layouts  5.43 us (5%)
    pallas_call x1, Pallas kernels, step_call(): pl.pallas_call(step_kernel, out_shape=[sds(x.shape, BF16), sds(x.shape, B...  110 us
    unnamed x13, local copies, waits for them, and re-layouts  5.43 us

profile of v2, /device:TPU:7, one launch (start us, length us, event | category | flops | bytes accessed | tf_op | source)
XLA Modules:
  0.0 115.8 jit_solution(7696537245655044711)
XLA Ops:
  0.6 109.7 %step.1 = (bf16[9,32,2048]{2,1,0:T(8,128)(2,1)}, bf16[9,32,2048]{2,1,0:T(8,128)(2,1)}, bf16[3,128,128]{2,1,0:T(8,128)(2,1)}, bf16[128,128]{1,0:T(8,128)(2,1)}, bf16[3,128,128]{2,1,0:T(8,128)(2,1)}) custom-call(bf16[9,32,2048]{2,1,0:T(8,128)(2,1)} %bitcast.5, bf16[9,32,2048]{2,1,0:T(8,128)(2,1)} %bitcast.6, f32[3,32]{1,0:T(4,128)} %gain_loc.1, ...), custom_call_target="tpu_custom_call" | custom-call | tf_op jit(solution)/shard_map/step/pallas_call | solution.py:409
  110.4 0.0 copy-start
  110.4 2.5 %copy.18 = bf16[2048,9,32]{0,2,1:T(8,128)(2,1)} copy(bf16[2048,9,32]{0,2,1:T(8,128)(2,1)} %bitcast.8) | data formatting | bytes 2359296
  112.9 0.0 copy-done
  112.9 0.0 copy-start.2
  112.9 0.0 copy-start.3
  112.9 0.0 copy-start.1
  112.9 1.0 copy.19
  113.9 0.0 copy-done.2
  113.9 0.6 copy.20
  114.6 0.0 copy-done.3
  114.6 0.6 copy.21
  115.2 0.0 copy-done.1
  115.2 0.6 copy.22
Async XLA Ops:
  110.4 2.5 %copy-start = (bf16[9,32,2048]{2,1,0:T(8,128)(2,1)S(1)}, bf16[9,32,2048]{2,1,0:T(8,128)(2,1)}, u32[]{:S(2)}) copy-start(bf16[9,32,2048]{2,1,0:T(8,128)(2,1)} %get-tuple-element.11) | copy-start | bytes 3538948
  112.9 1.0 copy-start.2
  112.9 1.7 %copy-start.3 = (bf16[128,128]{1,0:T(8,128)(2,1)S(1)}, bf16[128,128]{1,0:T(8,128)(2,1)}, u32[]{:S(2)}) copy-start(bf16[128,128]{1,0:T(8,128)(2,1)} %get-tuple-element.23) | copy-start | bytes 98308
  112.9 2.3 %copy-start.1 = (bf16[3,128,128]{2,1,0:T(8,128)(2,1)S(1)}, bf16[3,128,128]{2,1,0:T(8,128)(2,1)}, u32[]{:S(2)}) copy-start(bf16[3,128,128]{2,1,0:T(8,128)(2,1)} %get-tuple-element.24) | copy-start | bytes 294916

commit v3 on v2

--- a/solution.py
+++ b/solution.py
@@ -1,4 +1,3 @@
-import functools
 import jax
 import jax.numpy as jnp
 from jax import lax
@@ -131,7 +130,7 @@
             cols = part(tgt * BLOCKS + b, BLK)
             for i, (src, dst) in enumerate(((x_loc, x_all), (g_loc, g_all))):
                 acts[b].append(remote(src.at[:, :, cols], dst.at[:, part(me, SLICE), part(b, BLK)], act_send.at[b, d, i], act_recv.at[b, d, i], peer))
-        start(acts[b])
+    start(acts[0])
     local = [pltpu.make_async_copy(src, dst, loc_sem.at[i]) for i, (src, dst) in enumerate(
         pieces + [(x_loc.at[:, :, part(me, atoms)], x_all.at[:, part(me, SLICE), :]), (g_loc.at[:, :, part(me, atoms)], g_all.at[:, part(me, SLICE), :])])]
     start(local)
@@ -329,6 +328,9 @@
             r5[part(z, TILE), :] = fin[...]
 
     first, second = pl.ds(0, BLK), pl.ds(BLK, BLK)
+    for c in acts[0]:
+        c.wait_send()
+    start(acts[1])
     arrive(acts[0])
     stats = norm(first)
     up(first)
@@ -384,7 +386,7 @@
         d_down[degree] = r7[(TP + degree) * CH:(TP + degree + 1) * CH, :]
     d_gate[...] = r7[DEGS * CH:TP * CH, :]
     finished = wx + gx + wy + wc + c1 + c5 + c6
-    for group_of in acts + c2 + c3 + c4:
+    for group_of in [acts[1]] + c2 + c3 + c4:
         finished = finished + group_of
     for b in range(BLOCKS):
         for i in range(2):

time: 116 us -> 114 us (0.983)
  Pallas kernels: 110 us -> 107 us
    pallas_call x1, Pallas kernels: 110 us -> 107 us  [step_call(): pl.pallas_call(step_kernel, out_shape=[sds(x.shape, BF16), sds(x.shape, B...]
where the time goes in v3:
time: 114 us; the launch traced here: 113 us
  Pallas kernels  107 us (94%)
  local copies, waits for them, and re-layouts  5.43 us (5%)
    pallas_call x1, Pallas kernels, step_call(): pl.pallas_call(step_kernel, out_shape=[sds(x.shape, BF16), sds(x.shape, B...  107 us
    unnamed x13, local copies, waits for them, and re-layouts  5.43 us

profile of v3, /device:TPU:7, one launch (start us, length us, event | category | flops | bytes accessed | tf_op | source)
XLA Modules:
  0.0 113.5 jit_solution(5194948471843627576)
XLA Ops:
  0.6 107.4 %step.1 = (bf16[9,32,2048]{2,1,0:T(8,128)(2,1)}, bf16[9,32,2048]{2,1,0:T(8,128)(2,1)}, bf16[3,128,128]{2,1,0:T(8,128)(2,1)}, bf16[128,128]{1,0:T(8,128)(2,1)}, bf16[3,128,128]{2,1,0:T(8,128)(2,1)}) custom-call(bf16[9,32,2048]{2,1,0:T(8,128)(2,1)} %bitcast.5, bf16[9,32,2048]{2,1,0:T(8,128)(2,1)} %bitcast.6, f32[3,32]{1,0:T(4,128)} %gain_loc.1, ...), custom_call_target="tpu_custom_call" | custom-call | tf_op jit(solution)/shard_map/step/pallas_call | solution.py:411
  108.0 0.0 copy-start
  108.0 2.5 %copy.18 = bf16[2048,9,32]{0,2,1:T(8,128)(2,1)} copy(bf16[2048,9,32]{0,2,1:T(8,128)(2,1)} %bitcast.8) | data formatting | bytes 2359296
  110.6 0.0 copy-done
  110.6 0.0 copy-start.2
  110.6 0.0 copy-start.3
  110.6 0.0 copy-start.1
  110.6 1.0 copy.19
  111.6 0.0 copy-done.2
  111.6 0.6 copy.20
  112.2 0.0 copy-done.3
  112.2 0.6 copy.21
  112.8 0.0 copy-done.1
  112.8 0.6 copy.22
Async XLA Ops:
  108.0 2.5 %copy-start = (bf16[9,32,2048]{2,1,0:T(8,128)(2,1)S(1)}, bf16[9,32,2048]{2,1,0:T(8,128)(2,1)}, u32[]{:S(2)}) copy-start(bf16[9,32,2048]{2,1,0:T(8,128)(2,1)} %get-tuple-element.11) | copy-start | bytes 3538948
  110.6 1.0 copy-start.2
  110.6 1.7 %copy-start.3 = (bf16[128,128]{1,0:T(8,128)(2,1)S(1)}, bf16[128,128]{1,0:T(8,128)(2,1)}, u32[]{:S(2)}) copy-start(bf16[128,128]{1,0:T(8,128)(2,1)} %get-tuple-element.23) | copy-start | bytes 98308
  110.6 2.3 %copy-start.1 = (bf16[3,128,128]{2,1,0:T(8,128)(2,1)S(1)}, bf16[3,128,128]{2,1,0:T(8,128)(2,1)}, u32[]{:S(2)}) copy-start(bf16[3,128,128]{2,1,0:T(8,128)(2,1)} %get-tuple-element.24) | copy-start | bytes 294916

commit v4 on v3

--- a/solution.py
+++ b/solution.py
@@ -130,7 +130,7 @@
             cols = part(tgt * BLOCKS + b, BLK)
             for i, (src, dst) in enumerate(((x_loc, x_all), (g_loc, g_all))):
                 acts[b].append(remote(src.at[:, :, cols], dst.at[:, part(me, SLICE), part(b, BLK)], act_send.at[b, d, i], act_recv.at[b, d, i], peer))
-    start(acts[0])
+    start(acts[0][0::2])
     local = [pltpu.make_async_copy(src, dst, loc_sem.at[i]) for i, (src, dst) in enumerate(
         pieces + [(x_loc.at[:, :, part(me, atoms)], x_all.at[:, part(me, SLICE), :]), (g_loc.at[:, :, part(me, atoms)], g_all.at[:, part(me, SLICE), :])])]
     start(local)
@@ -155,6 +155,7 @@
     wy = [remote(whole(eighth), whole(eighth), wy_send.at[d, i], wy_recv.at[d, i], peer)
           for d, peer in enumerate(y_peers) for i, whole in enumerate(wholes)]
     start(wy)
+    start(acts[0][1::2])
     arrive(gx)
     for t in range(TP):
         pad_s[2, t * NZ:t * NZ + DEGS, 0:SLICE] = gain_x[t]
@@ -276,21 +277,23 @@
 
     outs = ((out_all, out_loc), (dx_all, dx_loc))
 
-    def out_copies(b, i):
+    def out_copies(b, i, third):
         src, dst = outs[i]
+        coefs = slice(third * DEGS, (third + 1) * DEGS)
         cols = part(me * BLOCKS + b, BLK)
-        return [remote(src.at[:, part(lax.rem(me + d, TP), SLICE), part(b, BLK)], dst.at[:, :, cols],
-                       o_send.at[b, i, d - 1], o_recv.at[b, i, d - 1], x_peers[d - 1]) for d in x_dist]
+        return [remote(src.at[coefs, part(lax.rem(me + d, TP), SLICE), part(b, BLK)], dst.at[coefs, :, cols],
+                       o_send.at[b, i, third, d - 1], o_recv.at[b, i, third, d - 1], x_peers[d - 1]) for d in x_dist]
 
     def out_local(b, i):
         src, dst = outs[i]
         return pltpu.make_async_copy(src.at[:, part(me, SLICE), part(b, BLK)], dst.at[:, :, part(me * BLOCKS + b, BLK)], oloc_sem.at[b, i])
 
-    sent = [[out_copies(b, i) for i in range(2)] for b in range(BLOCKS)]
+    sent = [[[out_copies(b, i, third) for third in range(DEGS)] for i in range(2)] for b in range(BLOCKS)]
     kept = [[out_local(b, i) for i in range(2)] for b in range(BLOCKS)]
 
     def send_out(b, i):
-        start(sent[b][i])
+        for third in range(DEGS):
+            start(sent[b][i][third])
         kept[b][i].start()
 
     half_rows = ROWS // 2
@@ -359,22 +362,28 @@
             sum_y(0)
         weight_grads(t, second)
         start([c1[t]])
+    sum_y(1)
     down(second)
-    send_out(1, 0)
     sum_core(TP - 1)
-    sum_y(1)
+    start(sent[1][0][0])
+    kept[1][0].start()
     norm_back(second, *stats)
+    kept[1][1].start()
+    sum_y(2)
     sum_z(0)
-    sum_y(2)
+    start(sent[1][0][1])
     sum_z(1)
+    sum_y(3)
+    start(sent[1][0][2])
+    start(sent[1][1][0])
+    sum_z(2)
     sum_x(0)
-    sum_y(3)
-    sum_z(2)
     sum_x(1)
     sum_z(3)
-    send_out(1, 1)
+    start(sent[1][1][1])
     sum_x(2)
     sum_x(3)
+    start(sent[1][1][2])
     arrive(c5)
     slot = part(core * TP + y, EIGHTH)
     c6 = [remote(r5.at[0:EIGHTH, :], r7.at[slot, :], s6.at[i], q6.at[i], yc_peers[i]) for i in range(len(group))]
@@ -390,9 +399,10 @@
         finished = finished + group_of
     for b in range(BLOCKS):
         for i in range(2):
-            arrive(sent[b][i])
             kept[b][i].wait()
-            finished = finished + sent[b][i]
+            for third in range(DEGS):
+                arrive(sent[b][i][third])
+                finished = finished + sent[b][i][third]
     for c in finished:
         c.wait_send()
 
@@ -424,20 +434,44 @@
             v((NZ * TILE, CH), BF16), v((ROWS, CH), BF16),
             dma((BLOCKS, peers, 2)), dma((BLOCKS, peers, 2)), dma((peers, 3)), dma((peers, 3)), dma((peers, 3)), dma((peers, 3)), dma((3,)), dma((3,)),
             dma((peers,)), dma((peers,)), dma((5,)),
-            dma((BLOCKS, 2, peers)), dma((BLOCKS, 2, peers)), dma((BLOCKS, 2)),
+            dma((BLOCKS, 2, DEGS, peers)), dma((BLOCKS, 2, DEGS, peers)), dma((BLOCKS, 2)),
             dma((TP,)), dma((TP,)), dma((TP, peers)), dma((TP, peers)), dma((TP, zs)), dma((TP, zs)), dma((TP, peers)), dma((TP, peers)),
             dma((zs,)), dma((zs,)), dma((zs,)), dma((zs,))],
         compiler_params=pltpu.CompilerParams(collective_id=0, has_side_effects=True, vmem_limit_bytes=VMEM_LIMIT), name="step",
     )(x, g, gain, up, gate, down, tog, frg)
 
 
+def store_kernel(*refs):
+    count = (len(refs) - 2) // 3
+    sources, results, bufs = refs[:count], refs[count:2 * count], refs[2 * count:3 * count]
+    in_sem, out_sem = refs[3 * count:]
+    loads = [pltpu.make_async_copy(src, buf, in_sem.at[i]) for i, (src, buf) in enumerate(zip(sources, bufs))]
+    stores = [pltpu.make_async_copy(buf, dst, out_sem.at[i]) for i, (buf, dst) in enumerate(zip(bufs, results))]
+    start(loads)
+    for load, store in zip(loads, stores):
+        load.wait()
+        store.start()
+    for store in stores:
+        store.wait()
+
+
+def store_call(*arrays):
+    hbm = pl.BlockSpec(memory_space=pl.ANY)
+    count = len(arrays)
+    return pl.pallas_call(
+        store_kernel, out_shape=[jax.ShapeDtypeStruct(a.shape, a.dtype) for a in arrays], in_specs=[hbm] * count, out_specs=[hbm] * count,
+        scratch_shapes=[pltpu.VMEM(a.shape, a.dtype) for a in arrays] + [pltpu.SemaphoreType.DMA((count,))] * 2,
+        compiler_params=pltpu.CompilerParams(vmem_limit_bytes=VMEM_LIMIT), name="store",
+    )(*arrays)
+
+
 def solution(mesh):
     act = P('dp', None, 'tp')
     in_specs = (act, P(None, 'tp'), P(None, None, 'tp'), P(None, 'tp'), P(None, 'tp', None), P(None, None), P(None, None), act)
     out_specs = (act, act, P(None, None, 'tp'), P(None, 'tp'), P(None, 'tp', None))
 
     def local_step(x, gain, up, gate, down, tog, frg, g):
-        out, dx, d_up, d_gate, d_down = step_call(x.transpose(1, 2, 0), g.transpose(1, 2, 0), gain, up, gate, down, tog, frg.T)
+        out, dx, d_up, d_gate, d_down = store_call(*step_call(x.transpose(1, 2, 0), g.transpose(1, 2, 0), gain, up, gate, down, tog, frg.T))
         return out.transpose(2, 0, 1), dx.transpose(2, 0, 1), d_up, d_gate, d_down
 
     return jax.shard_map(local_step, mesh=mesh, in_specs=in_specs, out_specs=out_specs, check_vma=False)

time: 114 us -> 110 us (0.965)
  the two profiles are of different devices: /device:TPU:7 before, /device:TPU:5 now
where the time goes in v4:
time: 110 us
  Pallas kernels  109 us (99%)
    pallas_call x1, Pallas kernels, step_call(): pl.pallas_call(step_kernel, out_shape=[sds(x.shape, BF16), sds(x.shape, B...  106 us
    pallas_call x1, Pallas kernels, store_call(): pl.pallas_call(store_kernel, out_shape=[jax.ShapeDtypeStruct(a.shape, a.d...  2.82 us

profile of v4, /device:TPU:5, one launch (start us, length us, event | category | flops | bytes accessed | tf_op | source)
XLA Modules:
  0.0 109.8 jit_solution(10049045095546486893)
XLA Ops:
  0.6 106.4 %step.1 = (bf16[9,32,2048]{2,1,0:T(8,128)(2,1)}, bf16[9,32,2048]{2,1,0:T(8,128)(2,1)}, bf16[3,128,128]{2,1,0:T(8,128)(2,1)}, bf16[128,128]{1,0:T(8,128)(2,1)}, bf16[3,128,128]{2,1,0:T(8,128)(2,1)}) custom-call(bf16[9,32,2048]{2,1,0:T(8,128)(2,1)} %bitcast.5, bf16[9,32,2048]{2,1,0:T(8,128)(2,1)} %bitcast.6, f32[3,32]{1,0:T(4,128)} %gain_loc.1, ...), custom_call_target="tpu_custom_call" | custom-call | tf_op jit(solution)/shard_map/step/pallas_call | solution.py:421
  107.0 2.8 %store.1 = (bf16[9,32,2048]{2,1,0:T(8,128)(2,1)}, bf16[9,32,2048]{2,1,0:T(8,128)(2,1)}, bf16[3,128,128]{2,1,0:T(8,128)(2,1)}, bf16[128,128]{1,0:T(8,128)(2,1)}, bf16[3,128,128]{2,1,0:T(8,128)(2,1)}) custom-call(bf16[9,32,2048]{2,1,0:T(8,128)(2,1)} %get-tuple-element.15.refs_0_, bf16[9,32,2048]{2,1,0:T(8,128)(2,1)} %get-tuple-element.16.refs_1_, ...), custom_call_target="tpu_custom_call" | custom-call | tf_op jit(solution)/shard_map/store/pallas_call | solution.py:461

commit v5 on v4

--- a/solution.py
+++ b/solution.py
@@ -44,11 +44,36 @@
     return jnp.where(iota(shape, 0) // row_div == iota(shape, 1) // col_div, 1.0, 0.0).astype(BF16)
 
 
-def spread(table, rows, row_div, cols, col_div):
-    left = mm(one_hot((rows, CH), row_div, 1), table).astype(BF16)
-    full = mm(left, one_hot((CH, cols), 1, col_div))
-    same = iota((rows, cols), 0) % SUB == iota((rows, cols), 1) % SUB
-    return jnp.where(same, full, 0.0)
+def point_of(row):
+    main = row < HID
+    point = jnp.where(main, (row % BLK) // NZ, SLICE + (row % SLICE) // NZ)
+    half = jnp.where(main, row // BLK, (row % 64) // SLICE)
+    return point, half
+
+
+def spread_out(table_t, cols):
+    point, half = point_of(iota((GRID_ROWS, CH), 0))
+    left = mm(jnp.where(point == iota((GRID_ROWS, CH), 1), 1.0, 0.0).astype(BF16), table_t).astype(BF16)
+    full = mm(left, one_hot((CH, cols), 1, SUB))
+    row = iota((GRID_ROWS, cols), 0)
+    same = point_of(row)[1] * NZ + row % NZ == iota((GRID_ROWS, cols), 1) % SUB
+    return jnp.where(same, 0.5 * full, 0.0).astype(BF16)
+
+
+def spread_back(table, rows):
+    left = mm(one_hot((rows, CH), NZ, 1), table).astype(BF16)
+    full = mm(left, one_hot((CH, BLK), 1, NZ))
+    return jnp.where(iota((rows, BLK), 0) % NZ == iota((rows, BLK), 1) % NZ, full, 0.0).astype(BF16)
+
+
+def spread_last(table, rows):
+    row, col = iota((2 * rows, CH), 0), iota((2 * rows, CH), 1)
+    r2, c2 = iota((2 * rows, CH), 0), iota((2 * rows, CH), 1)
+    left = mm(jnp.where((r2 % rows) // NZ == c2, 1.0, 0.0).astype(BF16), table).astype(BF16)
+    pick = jnp.where(iota((CH, CH), 0) == SLICE + (iota((CH, CH), 1) % SLICE) // NZ, 1.0, 0.0).astype(BF16)
+    full = mm(left, pick)
+    same = (row % NZ == col % NZ) & (row // rows == col // SLICE)
+    return jnp.where(same, full, 0.0).astype(BF16)
 
 
 def degree_of(coef):
@@ -86,7 +111,10 @@
         c.wait_recv()
 
 
-CHUNK = 144
+CHUNK = 288
+KROWS = 144
+ZROWS = 64
+YROWS = 72
 GROUPS = HID // SUB
 BLOCKS = 2
 
@@ -94,12 +122,14 @@
 def step_kernel(x_loc, g_loc, gain_loc, up_loc, gate_loc, down_loc, tog_ref, frg_ref,
                 out_loc, dx_loc, d_up, d_gate, d_down,
                 x_all, g_all, gain_x, up_all, gate_all, down_all, out_all, dx_all, wg, pad_s, gain_b,
-                wup_t, wgate_t, wdown_t, kg, kf, kft, kgt, n_s, y_s, dm_s, m_s, dy_s, da_s, dn_s, sb0, sb1, db0, db1,
-                r1, a1, r2, a2, r3, a3, r4, fin, r5, r7,
+                wup_t, wgate_t, wdown_t, kg, kf, kft, kgt, kftl, kgtl, n_s, y_s, dm_s, m_s, dy_s, da_s, dn0_s, dn1_s, sb0, sb1, db0, db1,
+                r1, a1, r2, a2, r3, a3, r4, fin, r5, r7, gain_v, tog_v, frg_v, small_sem,
                 act_send, act_recv, wx_send, wx_recv, wy_send, wy_recv, wc_send, wc_recv, gain_send, gain_recv, loc_sem,
                 o_send, o_recv, oloc_sem, s1, q1, s2, q2, s3, q3, s4, q4, s5, q5, s6, q6):
     me, z, y, core = places()
     atoms = x_all.shape[2]
+    small = [pltpu.make_async_copy(src, dst, small_sem.at[i]) for i, (src, dst) in enumerate(((gain_loc, gain_v), (tog_ref, tog_v), (frg_ref, frg_v)))]
+    start(small)
     pair = {"dp": dp_index(z, y, 1 - core)}
     x_dist = list(range(1, TP))
     x_peers = [{"tp": lax.rem(me + d, TP)} for d in x_dist]
@@ -136,18 +166,22 @@
     start(local)
 
     pad_s[...] = jnp.zeros(pad_s.shape, F32)
-    pad_s[0, 0:COEFS, 0:PTS] = tog_ref[...]
-    pad_s[1, 0:COEFS - 1, 0:PTS] = frg_ref[...]
+    for c in small:
+        c.wait()
+    pad_s[0, 0:COEFS, 0:PTS] = tog_v[...]
+    pad_s[1, 0:COEFS - 1, 0:PTS] = frg_v[...]
     tog, tog_t = pad_s[0].astype(BF16), pad_s[0].T.astype(BF16)
     frg_t, frg = pad_s[1].astype(BF16), pad_s[1].T.astype(BF16)
-    kg[...] = (0.5 * spread(tog_t, GRID_ROWS, SUB, BLK, SUB)).astype(BF16)
-    kf[...] = (0.5 * spread(frg, GRID_ROWS, SUB, CH, SUB)).astype(BF16)
-    kft[...] = spread(frg_t, CH, SUB, GRID_PAD, SUB).astype(BF16)
-    kgt[...] = spread(tog, CHUNK, SUB, GRID_PAD, SUB).astype(BF16)
+    kg[...] = spread_out(tog_t, BLK)
+    kf[...] = spread_out(frg, CH)
+    kft[...] = spread_back(frg_t, ZROWS)
+    kgt[...] = spread_back(tog, YROWS)
+    kftl[...] = spread_last(frg_t, ZROWS)
+    kgtl[...] = spread_last(tog, YROWS)
     for buf in (sb0, sb1, db0, db1):
         buf[GRID_ROWS:GRID_PAD, :] = jnp.zeros((GRID_PAD - GRID_ROWS, BLK), BF16)
     wg[...] = jnp.zeros(wg.shape, F32)
-    gain_x[me] = gain_loc[...]
+    gain_x[me] = gain_v[...]
     for c in local:
         c.wait()
     arrive(wx)
@@ -194,12 +228,14 @@
         return mean_s, inv_s, inv_v
 
     def up(lanes):
-        def up_step(coef, carry):
-            degree = degree_of(coef)
-            y_s[coef] = mm(wup_t[degree], n_s[coef]).astype(BF16)
-            dm_s[coef] = mm(down_all[degree].reshape(HID, CH), g_all[coef, :, lanes]).astype(BF16)
+        def up_step(i, carry):
+            for k in range(DEGS):
+                coef = i * DEGS + k
+                degree = degree_of(coef)
+                y_s[coef] = mm(wup_t[degree], n_s[coef]).astype(BF16)
+                dm_s[coef] = mm(down_all[degree].reshape(HID, CH), g_all[coef, :, lanes]).astype(BF16)
             return carry
-        lax.fori_loop(0, COEFS, up_step, 0)
+        lax.fori_loop(0, DEGS, up_step, 0)
 
         def gate_step(i, carry):
             rows = part(i, CH)
@@ -215,10 +251,10 @@
 
     def expand(j, s_buf, du_buf):
         rows = part(j, SUB)
-        yj = y_s[:, rows, :].reshape(CHUNK, BLK)
+        yj = y_s[:, rows, :].reshape(KROWS, BLK)
         dzj = dm_s[1:, rows, :].reshape(CH, BLK)
         for r0 in range(0, GRID_ROWS, CHUNK):
-            half = mm(kg[r0:r0 + CHUNK, 0:CHUNK], yj).astype(BF16).astype(F32)
+            half = mm(kg[r0:r0 + CHUNK, 0:KROWS], yj).astype(BF16).astype(F32)
             dval = mm(kf[r0:r0 + CHUNK, :], dzj).astype(BF16).astype(F32)
             th = jnp.tanh(half)
             plus = 1.0 + th
@@ -226,10 +262,15 @@
             s_buf[r0:r0 + CHUNK, :] = val.astype(BF16)
             du_buf[r0:r0 + CHUNK, :] = (dval * (plus + val * (1.0 - th))).astype(BF16)
 
+    def halves(back, last, buf, rows):
+        low = mm(last[...], buf[HID:GRID_PAD, :])
+        sums = [mm(back[...], buf[h * BLK:(h + 1) * BLK, :]) + low[h * rows:(h + 1) * rows, :] for h in range(2)]
+        return jnp.concatenate([v.reshape(rows // NZ, NZ, BLK) for v in sums], axis=1).astype(BF16)
+
     def contract(j, s_buf, du_buf):
         rows = part(j, SUB)
-        m_s[1:, rows, :] = mm(kft[...], s_buf[...]).astype(BF16).reshape(COEFS - 1, SUB, BLK)
-        dy_s[:, rows, :] = mm(kgt[...], du_buf[...]).astype(BF16).reshape(COEFS, SUB, BLK)
+        m_s[1:, rows, :] = halves(kft, kftl, s_buf, ZROWS)
+        dy_s[:, rows, :] = halves(kgt, kgtl, du_buf, YROWS)
 
     def grid_step(i, carry):
         expand(2 * i + 1, sb1, db1)
@@ -241,25 +282,25 @@
     def weight_grads(t, lanes):
         rows = part(t, CH)
 
-        def coef_step(coef, carry):
-            base = degree_of(coef) * CH
-            wg[t, part(degree_of(coef), CH), :] += mm_nt(n_s[coef], dy_s[coef, rows, :])
-            wg[t, part(degree_of(coef) + TP, CH), :] += mm_nt(m_s[coef, rows, :], g_all[coef, :, lanes])
+        for degree in range(DEGS):
+            coefs = range(degree * degree, (degree + 1) * (degree + 1))
+            wg[t, degree * CH:(degree + 1) * CH, :] += sum(mm_nt(n_s[c], dy_s[c, rows, :]) for c in coefs)
+            wg[t, (degree + TP) * CH:(degree + TP + 1) * CH, :] += sum(mm_nt(m_s[c, rows, :], g_all[c, :, lanes]) for c in coefs)
+        wg[t, DEGS * CH:TP * CH, :] += mm_nt(n_s[0], da_s[rows, :])
+
+    def down(lanes, dn_s):
+        def down_step(i, carry):
+            for k in range(DEGS):
+                coef = i * DEGS + k
+                degree = degree_of(coef)
+                xk = x_all[coef, :, lanes].astype(F32)
+                out_all[coef, :, lanes] = (xk + mm(wdown_t[degree], m_s[coef])).astype(BF16)
+                dn_s[coef] = mm(up_all[degree], dy_s[coef])
             return carry
-        lax.fori_loop(0, COEFS, coef_step, 0)
-        wg[t, part(DEGS, CH), :] += mm_nt(n_s[0], da_s[rows, :])
-
-    def down(lanes):
-        def down_step(coef, carry):
-            degree = degree_of(coef)
-            xk = x_all[coef, :, lanes].astype(F32)
-            out_all[coef, :, lanes] = (xk + mm(wdown_t[degree], m_s[coef])).astype(BF16)
-            dn_s[coef] = mm(up_all[degree], dy_s[coef])
-            return carry
-        lax.fori_loop(0, COEFS, down_step, 0)
+        lax.fori_loop(0, DEGS, down_step, 0)
         dn_s[0] += mm(gate_all[...], da_s[...])
 
-    def norm_back(lanes, mean_s, inv_s, inv_v):
+    def norm_back(lanes, dn_s, mean_s, inv_s, inv_v):
         hat = (x_all[0, :, lanes].astype(F32) - mean_s) * inv_s
         dh = dn_s[0].astype(BF16).astype(F32) * gain_of(0)
         m1 = jnp.sum(dh, axis=0, keepdims=True) * (1.0 / CH)
@@ -335,14 +376,12 @@
         c.wait_send()
     start(acts[1])
     arrive(acts[0])
-    stats = norm(first)
+    stats0 = norm(first)
     up(first)
     expand(0, sb0, db0)
     lax.fori_loop(0, GROUPS // 2, grid_step, 0)
-    down(first)
+    down(first, dn0_s)
     send_out(0, 0)
-    norm_back(first, *stats)
-    send_out(0, 1)
 
     def grads_step(t, carry):
         weight_grads(t, first)
@@ -363,27 +402,21 @@
         weight_grads(t, second)
         start([c1[t]])
     sum_y(1)
-    down(second)
+    down(second, dn1_s)
     sum_core(TP - 1)
-    start(sent[1][0][0])
-    kept[1][0].start()
-    norm_back(second, *stats)
-    kept[1][1].start()
+    send_out(1, 0)
     sum_y(2)
+    norm_back(second, dn1_s, *stats)
     sum_z(0)
-    start(sent[1][0][1])
+    norm_back(first, dn0_s, *stats0)
     sum_z(1)
     sum_y(3)
-    start(sent[1][0][2])
-    start(sent[1][1][0])
+    send_out(1, 1)
     sum_z(2)
-    sum_x(0)
-    sum_x(1)
     sum_z(3)
-    start(sent[1][1][1])
-    sum_x(2)
-    sum_x(3)
-    start(sent[1][1][2])
+    send_out(0, 1)
+    for t in range(TP):
+        sum_x(t)
     arrive(c5)
     slot = part(core * TP + y, EIGHTH)
     c6 = [remote(r5.at[0:EIGHTH, :], r7.at[slot, :], s6.at[i], q6.at[i], yc_peers[i]) for i in range(len(group))]
@@ -421,17 +454,17 @@
     return pl.pallas_call(
         step_kernel,
         out_shape=[sds(x.shape, BF16), sds(x.shape, BF16), sds((DEGS, CH, CH), BF16), sds((CH, CH), BF16), sds((DEGS, CH, CH), BF16)],
-        in_specs=[hbm] * 2 + [vm] * 6, out_specs=[hbm] * 2 + [vm] * 3,
+        in_specs=[hbm] * 8, out_specs=[hbm] * 2 + [vm] * 3,
         scratch_shapes=[
             v(act, BF16), v(act, BF16), v((TP, DEGS, SLICE), F32), v((DEGS, CH, HID), BF16), v((CH, HID), BF16), v((DEGS, TP, CH, CH), BF16),
             v(act, BF16), v(act, BF16), v((TP, ROWS, CH), F32), v((DEGS, CH, CH), F32), v((DEGS, CH, BLK), F32),
             v((DEGS, HID, CH), BF16), v((HID, CH), BF16), v((DEGS, CH, HID), BF16),
-            v((GRID_ROWS, BLK), BF16), v((GRID_ROWS, CH), BF16), v((CH, GRID_PAD), BF16), v((CHUNK, GRID_PAD), BF16),
-            v((COEFS, CH, BLK), BF16), v(hid, BF16), v(hid, BF16), v(hid, BF16), v(hid, BF16), v((HID, BLK), BF16), v((COEFS, CH, BLK), F32),
+            v((GRID_ROWS, BLK), BF16), v((GRID_ROWS, CH), BF16), v((ZROWS, BLK), BF16), v((YROWS, BLK), BF16), v((2 * ZROWS, CH), BF16), v((2 * YROWS, CH), BF16),
+            v((COEFS, CH, BLK), BF16), v(hid, BF16), v(hid, BF16), v(hid, BF16), v(hid, BF16), v((HID, BLK), BF16), v((COEFS, CH, BLK), F32), v((COEFS, CH, BLK), F32),
             v((GRID_PAD, BLK), BF16), v((GRID_PAD, BLK), BF16), v((GRID_PAD, BLK), BF16), v((GRID_PAD, BLK), BF16),
             v((TP, ROWS // 2, CH), F32), v((TP, ROWS // 2, CH), F32), v((TP, peers, EIGHTH, CH), F32), v((TP, EIGHTH, CH), F32),
             v((TP, zs, TILE, CH), F32), v((TP, TILE, CH), F32), v((TP, peers, TILE, CH), F32), v((TILE, CH), BF16),
-            v((NZ * TILE, CH), BF16), v((ROWS, CH), BF16),
+            v((NZ * TILE, CH), BF16), v((ROWS, CH), BF16), v((DEGS, SLICE), F32), v((COEFS, PTS), F32), v((COEFS - 1, PTS), F32), dma((3,)),
             dma((BLOCKS, peers, 2)), dma((BLOCKS, peers, 2)), dma((peers, 3)), dma((peers, 3)), dma((peers, 3)), dma((peers, 3)), dma((3,)), dma((3,)),
             dma((peers,)), dma((peers,)), dma((5,)),
             dma((BLOCKS, 2, DEGS, peers)), dma((BLOCKS, 2, DEGS, peers)), dma((BLOCKS, 2)),

time: 110 us -> 97.5 us (0.89)
  Pallas kernels: 109 us -> 96.7 us
    pallas_call x1, Pallas kernels: 106 us -> 93.9 us  [step_call(): pl.pallas_call(step_kernel, out_shape=[sds(x.shape, BF16), sds(x.shape, B...]
where the time goes in v5:
time: 97.5 us; the launch traced here: 97.4 us
  Pallas kernels  96.7 us (99%)
    pallas_call x1, Pallas kernels, step_call(): pl.pallas_call(step_kernel, out_shape=[sds(x.shape, BF16), sds(x.shape, B...  93.9 us
    pallas_call x1, Pallas kernels, store_call(): pl.pallas_call(store_kernel, out_shape=[jax.ShapeDtypeStruct(a.shape, a.d...  2.82 us

profile of v5, /device:TPU:5, one launch (start us, length us, event | category | flops | bytes accessed | tf_op | source)
XLA Modules:
  0.0 97.4 jit_solution(9232902976332548563)
XLA Ops:
  0.6 93.9 %step.1 = (bf16[9,32,2048]{2,1,0:T(8,128)(2,1)}, bf16[9,32,2048]{2,1,0:T(8,128)(2,1)}, bf16[3,128,128]{2,1,0:T(8,128)(2,1)}, bf16[128,128]{1,0:T(8,128)(2,1)}, bf16[3,128,128]{2,1,0:T(8,128)(2,1)}) custom-call(bf16[9,32,2048]{2,1,0:T(8,128)(2,1)} %bitcast.5, bf16[9,32,2048]{2,1,0:T(8,128)(2,1)} %bitcast.6, f32[3,32]{1,0:T(4,128)} %gain_loc.1, ...), custom_call_target="tpu_custom_call" | custom-call | tf_op jit(solution)/shard_map/step/pallas_call | solution.py:454
  94.6 2.8 %store.1 = (bf16[9,32,2048]{2,1,0:T(8,128)(2,1)}, bf16[9,32,2048]{2,1,0:T(8,128)(2,1)}, bf16[3,128,128]{2,1,0:T(8,128)(2,1)}, bf16[128,128]{1,0:T(8,128)(2,1)}, bf16[3,128,128]{2,1,0:T(8,128)(2,1)}) custom-call(bf16[9,32,2048]{2,1,0:T(8,128)(2,1)} %get-tuple-element.15.refs_0_, bf16[9,32,2048]{2,1,0:T(8,128)(2,1)} %get-tuple-element.16.refs_1_, ...), custom_call_target="tpu_custom_call" | custom-call | tf_op jit(solution)/shard_map/store/pallas_call | solution.py:494

commit v6 on v5

--- a/solution.py
+++ b/solution.py
@@ -122,7 +122,7 @@
 def step_kernel(x_loc, g_loc, gain_loc, up_loc, gate_loc, down_loc, tog_ref, frg_ref,
                 out_loc, dx_loc, d_up, d_gate, d_down,
                 x_all, g_all, gain_x, up_all, gate_all, down_all, out_all, dx_all, wg, pad_s, gain_b,
-                wup_t, wgate_t, wdown_t, kg, kf, kft, kgt, kftl, kgtl, n_s, y_s, dm_s, m_s, dy_s, da_s, dn0_s, dn1_s, sb0, sb1, db0, db1,
+                wup_t, wgate_t, wdown_t, kg, kf, kft, kgt, kftl, kgtl, n_s, y_s, dm_s, m_s, dy_s, da_s, dn_s, stat_s, sb0, sb1, db0, db1,
                 r1, a1, r2, a2, r3, a3, r4, fin, r5, r7, gain_v, tog_v, frg_v, small_sem,
                 act_send, act_recv, wx_send, wx_recv, wy_send, wy_recv, wc_send, wc_recv, gain_send, gain_recv, loc_sem,
                 o_send, o_recv, oloc_sem, s1, q1, s2, q2, s3, q3, s4, q4, s5, q5, s6, q6):
@@ -152,15 +152,15 @@
           for d, peer in enumerate(x_peers) for i, (src, dst) in enumerate(pieces)]
     gx = [remote(gain_loc, gain_x.at[me], gain_send.at[d], gain_recv.at[d], peer) for d, peer in enumerate(x_peers)]
     start(wx + gx)
-    acts = []
-    for b in range(BLOCKS):
-        acts.append([])
+    def acts(b):
+        copies = []
         for d, peer in enumerate(x_peers):
-            tgt = lax.rem(me + d + 1, TP)
-            cols = part(tgt * BLOCKS + b, BLK)
+            cols = part(lax.rem(me + d + 1, TP) * BLOCKS + b, BLK)
             for i, (src, dst) in enumerate(((x_loc, x_all), (g_loc, g_all))):
-                acts[b].append(remote(src.at[:, :, cols], dst.at[:, part(me, SLICE), part(b, BLK)], act_send.at[b, d, i], act_recv.at[b, d, i], peer))
-    start(acts[0][0::2])
+                copies.append(remote(src.at[:, :, cols], dst.at[:, part(me, SLICE), part(b, BLK)], act_send.at[b, d, i], act_recv.at[b, d, i], peer))
+        return copies
+
+    start(acts(0)[0::2])
     local = [pltpu.make_async_copy(src, dst, loc_sem.at[i]) for i, (src, dst) in enumerate(
         pieces + [(x_loc.at[:, :, part(me, atoms)], x_all.at[:, part(me, SLICE), :]), (g_loc.at[:, :, part(me, atoms)], g_all.at[:, part(me, SLICE), :])])]
     start(local)
@@ -189,7 +189,7 @@
     wy = [remote(whole(eighth), whole(eighth), wy_send.at[d, i], wy_recv.at[d, i], peer)
           for d, peer in enumerate(y_peers) for i, whole in enumerate(wholes)]
     start(wy)
-    start(acts[0][1::2])
+    start(acts(0)[1::2])
     arrive(gx)
     for t in range(TP):
         pad_s[2, t * NZ:t * NZ + DEGS, 0:SLICE] = gain_x[t]
@@ -211,7 +211,7 @@
     def gain_of(coef):
         return gain_b[0 if coef == 0 else (1 if coef < TP else 2)]
 
-    def norm(lanes):
+    def norm(b, lanes):
         x0 = x_all[0, :, lanes].astype(F32)
         mean_s = jnp.sum(x0, axis=0, keepdims=True) * (1.0 / CH)
         cen = x0 - mean_s
@@ -225,7 +225,8 @@
         for coef in range(1, COEFS):
             xk = x_all[coef, :, lanes].astype(F32)
             n_s[coef] = ((xk * inv_v) * gain_of(coef)).astype(BF16)
-        return mean_s, inv_s, inv_v
+        for i, stat in enumerate((mean_s, inv_s, inv_v)):
+            stat_s[b, i:i + 1, :] = stat
 
     def up(lanes):
         def up_step(i, carry):
@@ -288,33 +289,37 @@
             wg[t, (degree + TP) * CH:(degree + TP + 1) * CH, :] += sum(mm_nt(m_s[c, rows, :], g_all[c, :, lanes]) for c in coefs)
         wg[t, DEGS * CH:TP * CH, :] += mm_nt(n_s[0], da_s[rows, :])
 
-    def down(lanes, dn_s):
+    def down(b, lanes):
         def down_step(i, carry):
             for k in range(DEGS):
                 coef = i * DEGS + k
                 degree = degree_of(coef)
                 xk = x_all[coef, :, lanes].astype(F32)
                 out_all[coef, :, lanes] = (xk + mm(wdown_t[degree], m_s[coef])).astype(BF16)
-                dn_s[coef] = mm(up_all[degree], dy_s[coef])
+                dn_s[b, coef] = mm(up_all[degree], dy_s[coef])
             return carry
         lax.fori_loop(0, DEGS, down_step, 0)
-        dn_s[0] += mm(gate_all[...], da_s[...])
-
-    def norm_back(lanes, dn_s, mean_s, inv_s, inv_v):
+        dn_s[b, 0] += mm(gate_all[...], da_s[...])
+
+    def norm_back(i, carry):
+        b = 1 - i
+        lanes = part(b, BLK)
+        mean_s, inv_s, inv_v = [stat_s[b, k:k + 1, :] for k in range(DEGS)]
         hat = (x_all[0, :, lanes].astype(F32) - mean_s) * inv_s
-        dh = dn_s[0].astype(BF16).astype(F32) * gain_of(0)
+        dh = dn_s[b, 0].astype(BF16).astype(F32) * gain_of(0)
         m1 = jnp.sum(dh, axis=0, keepdims=True) * (1.0 / CH)
         m2 = jnp.sum(dh * hat, axis=0, keepdims=True) * (1.0 / CH)
         dx_all[0, :, lanes] = (inv_s * (dh - m1 - hat * m2) + g_all[0, :, lanes].astype(F32)).astype(BF16)
         acc = jnp.zeros((CH, BLK), F32)
         for coef in range(1, COEFS):
             xk = x_all[coef, :, lanes].astype(F32)
-            acc = acc + (dn_s[coef].astype(BF16).astype(F32) * gain_of(coef)) * (xk * inv_v)
+            acc = acc + (dn_s[b, coef].astype(BF16).astype(F32) * gain_of(coef)) * (xk * inv_v)
         mv = jnp.sum(acc, axis=0, keepdims=True) * VEC_SCALE
         for coef in range(1, COEFS):
             xk = x_all[coef, :, lanes].astype(F32)
-            dh = dn_s[coef].astype(BF16).astype(F32) * gain_of(coef)
+            dh = dn_s[b, coef].astype(BF16).astype(F32) * gain_of(coef)
             dx_all[coef, :, lanes] = (inv_v * (dh - (xk * inv_v) * mv) + g_all[coef, :, lanes].astype(F32)).astype(BF16)
+        return carry
 
     outs = ((out_all, out_loc), (dx_all, dx_loc))
 
@@ -338,32 +343,40 @@
         kept[b][i].start()
 
     half_rows = ROWS // 2
-    c1 = [remote(wg.at[t, part(1 - core, half_rows), :], r1.at[t], s1.at[t], q1.at[t], pair) for t in range(TP)]
-    c2 = [[remote(a1.at[t, part(lax.rem(y + d, TP), EIGHTH), :], r2.at[t, d - 1], s2.at[t, d - 1], q2.at[t, d - 1], y_peers[d - 1]) for d in x_dist]
-          for t in range(TP)]
-    c3 = [[remote(a2.at[t, part(lax.rem(lax.rem(z + d, NZ), NZ - 1), TILE), :], r3.at[t, d - 1], s3.at[t, d - 1], q3.at[t, d - 1], z_peers[d - 1])
-           for d in range(1, NZ)] for t in range(TP)]
-    c4 = [[remote(a3.at[t], r4.at[t, d - 1], s4.at[t, d - 1], q4.at[t, d - 1], x_peers[d - 1]) for d in x_dist] for t in range(TP)]
+
+    def c1(t):
+        return remote(wg.at[t, part(1 - core, half_rows), :], r1.at[t], s1.at[t], q1.at[t], pair)
+
+    def c2(t):
+        return [remote(a1.at[t, part(lax.rem(y + d, TP), EIGHTH), :], r2.at[t, d - 1], s2.at[t, d - 1], q2.at[t, d - 1], y_peers[d - 1]) for d in x_dist]
+
+    def c3(t):
+        return [remote(a2.at[t, part(lax.rem(lax.rem(z + d, NZ), NZ - 1), TILE), :], r3.at[t, d - 1], s3.at[t, d - 1], q3.at[t, d - 1], z_peers[d - 1])
+                for d in range(1, NZ)]
+
+    def c4(t):
+        return [remote(a3.at[t], r4.at[t, d - 1], s4.at[t, d - 1], q4.at[t, d - 1], x_peers[d - 1]) for d in x_dist]
+
     c5 = [remote(fin, r5.at[part(z, TILE), :], s5.at[d - 1], q5.at[d - 1], z_peers[d - 1]) for d in range(1, NZ)]
 
     def sum_core(t):
-        arrive([c1[t]])
+        c1(t).wait_recv()
         a1[t] = wg[t, part(core, half_rows), :] + r1[t]
-        start(c2[t])
+        start(c2(t))
 
     def sum_y(t):
-        arrive(c2[t])
+        arrive(c2(t))
         a2[t] = (a1[t, part(y, EIGHTH), :] + r2[t, 0]) + (r2[t, 1] + r2[t, 2])
-        start(c3[t])
+        start(c3(t))
 
     def sum_z(t):
-        arrive(c3[t])
+        arrive(c3(t))
         own = a2[t, part(lax.rem(z, NZ - 1), TILE), :]
         a3[t] = ((own + r3[t, 0]) + (r3[t, 1] + r3[t, 2])) + ((r3[t, 3] + r3[t, 4]) + (r3[t, 5] + r3[t, 6]))
-        start(c4[t])
+        start(c4(t))
 
     def sum_x(t):
-        arrive(c4[t])
+        arrive(c4(t))
 
         @pl.when(me == t)
         def _():
@@ -371,44 +384,48 @@
             start(c5)
             r5[part(z, TILE), :] = fin[...]
 
-    first, second = pl.ds(0, BLK), pl.ds(BLK, BLK)
-    for c in acts[0]:
+    for c in acts(0):
         c.wait_send()
-    start(acts[1])
-    arrive(acts[0])
-    stats0 = norm(first)
-    up(first)
-    expand(0, sb0, db0)
-    lax.fori_loop(0, GROUPS // 2, grid_step, 0)
-    down(first, dn0_s)
-    send_out(0, 0)
-
-    def grads_step(t, carry):
-        weight_grads(t, first)
+    start(acts(1))
+    per = GROUPS // 2 // TP
+
+    def block_step(b, carry):
+        lanes = part(b, BLK)
+        arrive(acts(b))
+        norm(b, lanes)
+        up(lanes)
+        expand(0, sb0, db0)
+
+        def quarter_step(t, inner):
+            lax.fori_loop(t * per, (t + 1) * per, grid_step, 0)
+
+            @pl.when((b == 1) & (t > 0))
+            def _():
+                sum_core(t - 1)
+
+            @pl.when((b == 1) & (t == TP - 1))
+            def _():
+                sum_y(0)
+            weight_grads(t, lanes)
+
+            @pl.when(b == 1)
+            def _():
+                c1(t).start()
+            return inner
+        lax.fori_loop(0, TP, quarter_step, 0)
+        down(b, lanes)
+
+        @pl.when(b == 0)
+        def _():
+            send_out(0, 0)
         return carry
-    lax.fori_loop(0, TP, grads_step, 0)
-
-    arrive(acts[1])
-    stats = norm(second)
-    up(second)
-    expand(0, sb0, db0)
-    per = GROUPS // 2 // TP
-    for t in range(TP):
-        lax.fori_loop(t * per, (t + 1) * per, grid_step, 0)
-        if t > 0:
-            sum_core(t - 1)
-        if t == TP - 1:
-            sum_y(0)
-        weight_grads(t, second)
-        start([c1[t]])
-    sum_y(1)
-    down(second, dn1_s)
+    lax.fori_loop(0, BLOCKS, block_step, 0)
     sum_core(TP - 1)
     send_out(1, 0)
+    sum_y(1)
     sum_y(2)
-    norm_back(second, dn1_s, *stats)
+    lax.fori_loop(0, BLOCKS, norm_back, 0)
     sum_z(0)
-    norm_back(first, dn0_s, *stats0)
     sum_z(1)
     sum_y(3)
     send_out(1, 1)
@@ -427,9 +444,9 @@
         d_up[degree] = r7[degree * CH:(degree + 1) * CH, :]
         d_down[degree] = r7[(TP + degree) * CH:(TP + degree + 1) * CH, :]
     d_gate[...] = r7[DEGS * CH:TP * CH, :]
-    finished = wx + gx + wy + wc + c1 + c5 + c6
-    for group_of in [acts[1]] + c2 + c3 + c4:
-        finished = finished + group_of
+    finished = wx + gx + wy + wc + c5 + c6 + acts(1)
+    for t in range(TP):
+        finished = finished + [c1(t)] + c2(t) + c3(t) + c4(t)
     for b in range(BLOCKS):
         for i in range(2):
             kept[b][i].wait()
@@ -460,7 +477,7 @@
             v(act, BF16), v(act, BF16), v((TP, ROWS, CH), F32), v((DEGS, CH, CH), F32), v((DEGS, CH, BLK), F32),
             v((DEGS, HID, CH), BF16), v((HID, CH), BF16), v((DEGS, CH, HID), BF16),
             v((GRID_ROWS, BLK), BF16), v((GRID_ROWS, CH), BF16), v((ZROWS, BLK), BF16), v((YROWS, BLK), BF16), v((2 * ZROWS, CH), BF16), v((2 * YROWS, CH), BF16),
-            v((COEFS, CH, BLK), BF16), v(hid, BF16), v(hid, BF16), v(hid, BF16), v(hid, BF16), v((HID, BLK), BF16), v((COEFS, CH, BLK), F32), v((COEFS, CH, BLK), F32),
+            v((COEFS, CH, BLK), BF16), v(hid, BF16), v(hid, BF16), v(hid, BF16), v(hid, BF16), v((HID, BLK), BF16), v((BLOCKS, COEFS, CH, BLK), F32), v((BLOCKS, NZ, BLK), F32),
             v((GRID_PAD, BLK), BF16), v((GRID_PAD, BLK), BF16), v((GRID_PAD, BLK), BF16), v((GRID_PAD, BLK), BF16),
             v((TP, ROWS // 2, CH), F32), v((TP, ROWS // 2, CH), F32), v((TP, peers, EIGHTH, CH), F32), v((TP, EIGHTH, CH), F32),
             v((TP, zs, TILE, CH), F32), v((TP, TILE, CH), F32), v((TP, peers, TILE, CH), F32), v((TILE, CH), BF16),

time: 97.5 us -> 97.5 us (level)
  no operation moved by 1% of the time
where the time goes in v6:
time: 97.5 us; the launch traced here: 97.4 us
  Pallas kernels  96.7 us (99%)
    pallas_call x1, Pallas kernels, step_call(): pl.pallas_call(step_kernel, out_shape=[sds(x.shape, BF16), sds(x.shape, B...  93.9 us
    pallas_call x1, Pallas kernels, store_call(): pl.pallas_call(store_kernel, out_shape=[jax.ShapeDtypeStruct(a.shape, a.d...  2.82 us

profile of v6, /device:TPU:5, one launch (start us, length us, event | category | flops | bytes accessed | tf_op | source)
XLA Modules:
  0.0 97.4 jit_solution(16014972299046856240)
XLA Ops:
  0.6 93.9 %step.1 = (bf16[9,32,2048]{2,1,0:T(8,128)(2,1)}, bf16[9,32,2048]{2,1,0:T(8,128)(2,1)}, bf16[3,128,128]{2,1,0:T(8,128)(2,1)}, bf16[128,128]{1,0:T(8,128)(2,1)}, bf16[3,128,128]{2,1,0:T(8,128)(2,1)}) custom-call(bf16[9,32,2048]{2,1,0:T(8,128)(2,1)} %bitcast.5, bf16[9,32,2048]{2,1,0:T(8,128)(2,1)} %bitcast.6, f32[3,32]{1,0:T(4,128)} %gain_loc.1, ...), custom_call_target="tpu_custom_call" | custom-call | tf_op jit(solution)/shard_map/step/pallas_call | solution.py:471
  94.6 2.8 %store.1 = (bf16[9,32,2048]{2,1,0:T(8,128)(2,1)}, bf16[9,32,2048]{2,1,0:T(8,128)(2,1)}, bf16[3,128,128]{2,1,0:T(8,128)(2,1)}, bf16[128,128]{1,0:T(8,128)(2,1)}, bf16[3,128,128]{2,1,0:T(8,128)(2,1)}) custom-call(bf16[9,32,2048]{2,1,0:T(8,128)(2,1)} %get-tuple-element.15.refs_0_, bf16[9,32,2048]{2,1,0:T(8,128)(2,1)} %get-tuple-element.16.refs_1_, ...), custom_call_target="tpu_custom_call" | custom-call | tf_op jit(solution)/shard_map/store/pallas_call | solution.py:511

commit v7 on v6

--- a/solution.py
+++ b/solution.py
@@ -120,10 +120,10 @@
 
 
 def step_kernel(x_loc, g_loc, gain_loc, up_loc, gate_loc, down_loc, tog_ref, frg_ref,
-                out_loc, dx_loc, d_up, d_gate, d_down,
+                out_loc, dx_loc, r7,
                 x_all, g_all, gain_x, up_all, gate_all, down_all, out_all, dx_all, wg, pad_s, gain_b,
                 wup_t, wgate_t, wdown_t, kg, kf, kft, kgt, kftl, kgtl, n_s, y_s, dm_s, m_s, dy_s, da_s, dn_s, stat_s, sb0, sb1, db0, db1,
-                r1, a1, r2, a2, r3, a3, r4, fin, r5, r7, gain_v, tog_v, frg_v, small_sem,
+                r1, a1, r2, a2, r3, a3, r4, fin, r5, gain_v, tog_v, frg_v, small_sem,
                 act_send, act_recv, wx_send, wx_recv, wy_send, wy_recv, wc_send, wc_recv, gain_send, gain_recv, loc_sem,
                 o_send, o_recv, oloc_sem, s1, q1, s2, q2, s3, q3, s4, q4, s5, q5, s6, q6):
     me, z, y, core = places()
@@ -228,15 +228,21 @@
         for i, stat in enumerate((mean_s, inv_s, inv_v)):
             stat_s[b, i:i + 1, :] = stat
 
-    def up(lanes):
+    def up():
         def up_step(i, carry):
             for k in range(DEGS):
                 coef = i * DEGS + k
-                degree = degree_of(coef)
-                y_s[coef] = mm(wup_t[degree], n_s[coef]).astype(BF16)
-                dm_s[coef] = mm(down_all[degree].reshape(HID, CH), g_all[coef, :, lanes]).astype(BF16)
+                y_s[coef] = mm(wup_t[degree_of(coef)], n_s[coef]).astype(BF16)
             return carry
         lax.fori_loop(0, DEGS, up_step, 0)
+
+    def hidden_grads(b, lanes):
+        def grad_step(i, carry):
+            for k in range(DEGS):
+                coef = i * DEGS + k
+                dm_s[coef] = mm(down_all[degree_of(coef)].reshape(HID, CH), g_all[coef, :, lanes]).astype(BF16)
+            return carry
+        lax.fori_loop(0, DEGS, grad_step, 0)
 
         def gate_step(i, carry):
             rows = part(i, CH)
@@ -246,7 +252,7 @@
             val = half * plus
             m_s[0, rows, :] = val.astype(BF16)
             slope = 0.5 * (plus + val * (1.0 - th))
-            da_s[rows, :] = (dm_s[0, rows, :].astype(F32) * slope).astype(BF16)
+            da_s[b, rows, :] = (dm_s[0, rows, :].astype(F32) * slope).astype(BF16)
             return carry
         lax.fori_loop(0, TP, gate_step, 0)
 
@@ -268,56 +274,63 @@
         sums = [mm(back[...], buf[h * BLK:(h + 1) * BLK, :]) + low[h * rows:(h + 1) * rows, :] for h in range(2)]
         return jnp.concatenate([v.reshape(rows // NZ, NZ, BLK) for v in sums], axis=1).astype(BF16)
 
-    def contract(j, s_buf, du_buf):
+    def contract(b, j, s_buf, du_buf):
         rows = part(j, SUB)
         m_s[1:, rows, :] = halves(kft, kftl, s_buf, ZROWS)
-        dy_s[:, rows, :] = halves(kgt, kgtl, du_buf, YROWS)
-
-    def grid_step(i, carry):
+        dy_s[b, :, rows, :] = halves(kgt, kgtl, du_buf, YROWS)
+
+    def grid_step(i, b):
         expand(2 * i + 1, sb1, db1)
-        contract(2 * i, sb0, db0)
+        contract(b, 2 * i, sb0, db0)
         expand(jnp.minimum(2 * i + 2, GROUPS - 1), sb0, db0)
-        contract(2 * i + 1, sb1, db1)
-        return carry
-
-    def weight_grads(t, lanes):
+        contract(b, 2 * i + 1, sb1, db1)
+        return b
+
+    def weight_grads(b, t, lanes):
         rows = part(t, CH)
 
         for degree in range(DEGS):
             coefs = range(degree * degree, (degree + 1) * (degree + 1))
-            wg[t, degree * CH:(degree + 1) * CH, :] += sum(mm_nt(n_s[c], dy_s[c, rows, :]) for c in coefs)
+            wg[t, degree * CH:(degree + 1) * CH, :] += sum(mm_nt(n_s[c], dy_s[b, c, rows, :]) for c in coefs)
             wg[t, (degree + TP) * CH:(degree + TP + 1) * CH, :] += sum(mm_nt(m_s[c, rows, :], g_all[c, :, lanes]) for c in coefs)
-        wg[t, DEGS * CH:TP * CH, :] += mm_nt(n_s[0], da_s[rows, :])
-
-    def down(b, lanes):
+        wg[t, DEGS * CH:TP * CH, :] += mm_nt(n_s[0], da_s[b, rows, :])
+
+    def down(lanes):
         def down_step(i, carry):
             for k in range(DEGS):
                 coef = i * DEGS + k
-                degree = degree_of(coef)
                 xk = x_all[coef, :, lanes].astype(F32)
-                out_all[coef, :, lanes] = (xk + mm(wdown_t[degree], m_s[coef])).astype(BF16)
-                dn_s[b, coef] = mm(up_all[degree], dy_s[coef])
+                out_all[coef, :, lanes] = (xk + mm(wdown_t[degree_of(coef)], m_s[coef])).astype(BF16)
             return carry
         lax.fori_loop(0, DEGS, down_step, 0)
-        dn_s[b, 0] += mm(gate_all[...], da_s[...])
+
+    def norm_grads(b):
+        def norm_grad_step(i, carry):
+            for k in range(DEGS):
+                coef = i * DEGS + k
+                dn_s[coef] = mm(up_all[degree_of(coef)], dy_s[b, coef])
+            return carry
+        lax.fori_loop(0, DEGS, norm_grad_step, 0)
+        dn_s[0] += mm(gate_all[...], da_s[b])
 
     def norm_back(i, carry):
         b = 1 - i
+        norm_grads(b)
         lanes = part(b, BLK)
         mean_s, inv_s, inv_v = [stat_s[b, k:k + 1, :] for k in range(DEGS)]
         hat = (x_all[0, :, lanes].astype(F32) - mean_s) * inv_s
-        dh = dn_s[b, 0].astype(BF16).astype(F32) * gain_of(0)
+        dh = dn_s[0].astype(BF16).astype(F32) * gain_of(0)
         m1 = jnp.sum(dh, axis=0, keepdims=True) * (1.0 / CH)
         m2 = jnp.sum(dh * hat, axis=0, keepdims=True) * (1.0 / CH)
         dx_all[0, :, lanes] = (inv_s * (dh - m1 - hat * m2) + g_all[0, :, lanes].astype(F32)).astype(BF16)
         acc = jnp.zeros((CH, BLK), F32)
         for coef in range(1, COEFS):
             xk = x_all[coef, :, lanes].astype(F32)
-            acc = acc + (dn_s[b, coef].astype(BF16).astype(F32) * gain_of(coef)) * (xk * inv_v)
+            acc = acc + (dn_s[coef].astype(BF16).astype(F32) * gain_of(coef)) * (xk * inv_v)
         mv = jnp.sum(acc, axis=0, keepdims=True) * VEC_SCALE
         for coef in range(1, COEFS):
             xk = x_all[coef, :, lanes].astype(F32)
-            dh = dn_s[b, coef].astype(BF16).astype(F32) * gain_of(coef)
+            dh = dn_s[coef].astype(BF16).astype(F32) * gain_of(coef)
             dx_all[coef, :, lanes] = (inv_v * (dh - (xk * inv_v) * mv) + g_all[coef, :, lanes].astype(F32)).astype(BF16)
         return carry
 
@@ -391,13 +404,15 @@
 
     def block_step(b, carry):
         lanes = part(b, BLK)
-        arrive(acts(b))
+        arrive(acts(b)[0::2])
         norm(b, lanes)
-        up(lanes)
+        up()
+        arrive(acts(b)[1::2])
+        hidden_grads(b, lanes)
         expand(0, sb0, db0)
 
         def quarter_step(t, inner):
-            lax.fori_loop(t * per, (t + 1) * per, grid_step, 0)
+            lax.fori_loop(t * per, (t + 1) * per, grid_step, b)
 
             @pl.when((b == 1) & (t > 0))
             def _():
@@ -406,29 +421,31 @@
             @pl.when((b == 1) & (t == TP - 1))
             def _():
                 sum_y(0)
-            weight_grads(t, lanes)
+            weight_grads(b, t, lanes)
 
             @pl.when(b == 1)
             def _():
                 c1(t).start()
             return inner
         lax.fori_loop(0, TP, quarter_step, 0)
-        down(b, lanes)
 
         @pl.when(b == 0)
         def _():
+            down(lanes)
             send_out(0, 0)
         return carry
     lax.fori_loop(0, BLOCKS, block_step, 0)
+    down(pl.ds(BLK, BLK))
     sum_core(TP - 1)
     send_out(1, 0)
     sum_y(1)
+    norm_back(0, 0)
     sum_y(2)
-    lax.fori_loop(0, BLOCKS, norm_back, 0)
     sum_z(0)
-    sum_z(1)
     sum_y(3)
     send_out(1, 1)
+    norm_back(1, 0)
+    sum_z(1)
     sum_z(2)
     sum_z(3)
     send_out(0, 1)
@@ -438,12 +455,10 @@
     slot = part(core * TP + y, EIGHTH)
     c6 = [remote(r5.at[0:EIGHTH, :], r7.at[slot, :], s6.at[i], q6.at[i], yc_peers[i]) for i in range(len(group))]
     start(c6)
-    r7[slot, :] = r5[0:EIGHTH, :]
+    own = pltpu.make_async_copy(r5.at[0:EIGHTH, :], r7.at[slot, :], small_sem.at[0])
+    own.start()
     arrive(c6)
-    for degree in range(DEGS):
-        d_up[degree] = r7[degree * CH:(degree + 1) * CH, :]
-        d_down[degree] = r7[(TP + degree) * CH:(TP + degree + 1) * CH, :]
-    d_gate[...] = r7[DEGS * CH:TP * CH, :]
+    own.wait()
     finished = wx + gx + wy + wc + c5 + c6 + acts(1)
     for t in range(TP):
         finished = finished + [c1(t)] + c2(t) + c3(t) + c4(t)
@@ -458,7 +473,6 @@
 
 
 def step_call(x, g, gain, up, gate, down, tog, frg):
-    vm = pl.BlockSpec(memory_space=pltpu.VMEM)
     hbm = pl.BlockSpec(memory_space=pl.ANY)
     dma = pltpu.SemaphoreType.DMA
     v = pltpu.VMEM
@@ -470,18 +484,18 @@
     zs = NZ - 1
     return pl.pallas_call(
         step_kernel,
-        out_shape=[sds(x.shape, BF16), sds(x.shape, BF16), sds((DEGS, CH, CH), BF16), sds((CH, CH), BF16), sds((DEGS, CH, CH), BF16)],
-        in_specs=[hbm] * 8, out_specs=[hbm] * 2 + [vm] * 3,
+        out_shape=[sds(x.shape, BF16), sds(x.shape, BF16), sds((ROWS, CH), BF16)],
+        in_specs=[hbm] * 8, out_specs=[hbm] * 3,
         scratch_shapes=[
             v(act, BF16), v(act, BF16), v((TP, DEGS, SLICE), F32), v((DEGS, CH, HID), BF16), v((CH, HID), BF16), v((DEGS, TP, CH, CH), BF16),
             v(act, BF16), v(act, BF16), v((TP, ROWS, CH), F32), v((DEGS, CH, CH), F32), v((DEGS, CH, BLK), F32),
             v((DEGS, HID, CH), BF16), v((HID, CH), BF16), v((DEGS, CH, HID), BF16),
             v((GRID_ROWS, BLK), BF16), v((GRID_ROWS, CH), BF16), v((ZROWS, BLK), BF16), v((YROWS, BLK), BF16), v((2 * ZROWS, CH), BF16), v((2 * YROWS, CH), BF16),
-            v((COEFS, CH, BLK), BF16), v(hid, BF16), v(hid, BF16), v(hid, BF16), v(hid, BF16), v((HID, BLK), BF16), v((BLOCKS, COEFS, CH, BLK), F32), v((BLOCKS, NZ, BLK), F32),
+            v((COEFS, CH, BLK), BF16), v(hid, BF16), v(hid, BF16), v(hid, BF16), v((BLOCKS,) + hid, BF16), v((BLOCKS, HID, BLK), BF16), v((COEFS, CH, BLK), F32), v((BLOCKS, NZ, BLK), F32),
             v((GRID_PAD, BLK), BF16), v((GRID_PAD, BLK), BF16), v((GRID_PAD, BLK), BF16), v((GRID_PAD, BLK), BF16),
             v((TP, ROWS // 2, CH), F32), v((TP, ROWS // 2, CH), F32), v((TP, peers, EIGHTH, CH), F32), v((TP, EIGHTH, CH), F32),
             v((TP, zs, TILE, CH), F32), v((TP, TILE, CH), F32), v((TP, peers, TILE, CH), F32), v((TILE, CH), BF16),
-            v((NZ * TILE, CH), BF16), v((ROWS, CH), BF16), v((DEGS, SLICE), F32), v((COEFS, PTS), F32), v((COEFS - 1, PTS), F32), dma((3,)),
+            v((NZ * TILE, CH), BF16), v((DEGS, SLICE), F32), v((COEFS, PTS), F32), v((COEFS - 1, PTS), F32), dma((3,)),
             dma((BLOCKS, peers, 2)), dma((BLOCKS, peers, 2)), dma((peers, 3)), dma((peers, 3)), dma((peers, 3)), dma((peers, 3)), dma((3,)), dma((3,)),
             dma((peers,)), dma((peers,)), dma((5,)),
             dma((BLOCKS, 2, DEGS, peers)), dma((BLOCKS, 2, DEGS, peers)), dma((BLOCKS, 2)),
@@ -491,28 +505,34 @@
     )(x, g, gain, up, gate, down, tog, frg)
 
 
-def store_kernel(*refs):
-    count = (len(refs) - 2) // 3
-    sources, results, bufs = refs[:count], refs[count:2 * count], refs[2 * count:3 * count]
-    in_sem, out_sem = refs[3 * count:]
-    loads = [pltpu.make_async_copy(src, buf, in_sem.at[i]) for i, (src, buf) in enumerate(zip(sources, bufs))]
-    stores = [pltpu.make_async_copy(buf, dst, out_sem.at[i]) for i, (buf, dst) in enumerate(zip(bufs, results))]
+def store_kernel(out_in, dx_in, w_in, out, dx, d_up, d_gate, d_down, out_v, dx_v, w_v, in_sem, out_sem):
+    thirds = [pl.ds(i * DEGS, DEGS) for i in range(DEGS)]
+    moves = [((w_in, w_v), [(w_v.at[part(i, CH), :], d_up.at[i]) for i in range(DEGS)] + [(w_v.at[part(DEGS, CH), :], d_gate)]
+              + [(w_v.at[part(TP + i, CH), :], d_down.at[i]) for i in range(DEGS)])]
+    for src, buf, dst in ((out_in, out_v, out), (dx_in, dx_v, dx)):
+        moves = moves + [((src.at[k], buf.at[k]), [(buf.at[k], dst.at[k])]) for k in thirds]
+    loads = [pltpu.make_async_copy(*load, in_sem.at[i]) for i, (load, _) in enumerate(moves)]
     start(loads)
-    for load, store in zip(loads, stores):
+    stores = []
+    for load, (_, pairs) in zip(loads, moves):
         load.wait()
-        store.start()
+        for pair in pairs:
+            stores.append(pltpu.make_async_copy(*pair, out_sem.at[len(stores)]))
+            stores[-1].start()
     for store in stores:
         store.wait()
 
 
-def store_call(*arrays):
+def store_call(out, dx, w):
     hbm = pl.BlockSpec(memory_space=pl.ANY)
-    count = len(arrays)
+    sds = jax.ShapeDtypeStruct
+    mats = sds((DEGS, CH, CH), BF16)
+    v = pltpu.VMEM
     return pl.pallas_call(
-        store_kernel, out_shape=[jax.ShapeDtypeStruct(a.shape, a.dtype) for a in arrays], in_specs=[hbm] * count, out_specs=[hbm] * count,
-        scratch_shapes=[pltpu.VMEM(a.shape, a.dtype) for a in arrays] + [pltpu.SemaphoreType.DMA((count,))] * 2,
+        store_kernel, out_shape=[sds(out.shape, BF16), sds(dx.shape, BF16), mats, sds((CH, CH), BF16), mats], in_specs=[hbm] * 3, out_specs=[hbm] * 5,
+        scratch_shapes=[v(out.shape, BF16), v(dx.shape, BF16), v(w.shape, BF16), pltpu.SemaphoreType.DMA((7,)), pltpu.SemaphoreType.DMA((13,))],
         compiler_params=pltpu.CompilerParams(vmem_limit_bytes=VMEM_LIMIT), name="store",
-    )(*arrays)
+    )(out, dx, w)
 
 
 def solution(mesh):

time: 97.5 us -> 95.6 us (0.981)
  the two profiles are of different devices: /device:TPU:5 before, /device:TPU:3 now
where the time goes in v7:
time: 95.6 us; the launch traced here: 95.5 us
  Pallas kernels  94.9 us (99%)
    pallas_call x1, Pallas kernels, step_call(): pl.pallas_call(step_kernel, out_shape=[sds(x.shape, BF16), sds(x.shape, B...  92.2 us
    pallas_call x1, Pallas kernels, store_call(): pl.pallas_call(store_kernel, out_shape=[sds(out.shape, BF16), sds(dx.shap...  2.69 us

profile of v7, /device:TPU:3, one launch (start us, length us, event | category | flops | bytes accessed | tf_op | source)
XLA Modules:
  0.0 95.5 jit_solution(7149594800708785876)
XLA Ops:
  0.6 92.2 %step.1 = (bf16[9,32,2048]{2,1,0:T(8,128)(2,1)}, bf16[9,32,2048]{2,1,0:T(8,128)(2,1)}, bf16[896,128]{1,0:T(8,128)(2,1)}) custom-call(bf16[9,32,2048]{2,1,0:T(8,128)(2,1)} %bitcast.5, bf16[9,32,2048]{2,1,0:T(8,128)(2,1)} %bitcast.6, f32[3,32]{1,0:T(4,128)} %gain_loc.1, bf16[3,128,128]{2,1,0:T(8,128)(2,1)} %up_loc.1, bf16[128,128]{1,0:T(8,128)(2,1)} %gate_loc.1, ...), custom_call_target="tpu_custom_call" | custom-call | tf_op jit(solution)/shard_map/step/pallas_call | solution.py:485
  92.8 2.7 %store.1 = (bf16[9,32,2048]{2,1,0:T(8,128)(2,1)}, bf16[9,32,2048]{2,1,0:T(8,128)(2,1)}, bf16[3,128,128]{2,1,0:T(8,128)(2,1)}, bf16[128,128]{1,0:T(8,128)(2,1)}, bf16[3,128,128]{2,1,0:T(8,128)(2,1)}) custom-call(bf16[9,32,2048]{2,1,0:T(8,128)(2,1)} %get-tuple-element.13.out_in, bf16[9,32,2048]{2,1,0:T(8,128)(2,1)} %get-tuple-element.14.dx_in, ...), custom_call_target="tpu_custom_call" | custom-call | tf_op jit(solution)/shard_map/store/pallas_call | solution.py:531

commit v8 on v7

--- a/solution.py
+++ b/solution.py
@@ -113,6 +113,7 @@
 
 CHUNK = 288
 KROWS = 144
+UNROLL = 4
 ZROWS = 64
 YROWS = 72
 GROUPS = HID // SUB
@@ -254,7 +255,8 @@
             slope = 0.5 * (plus + val * (1.0 - th))
             da_s[b, rows, :] = (dm_s[0, rows, :].astype(F32) * slope).astype(BF16)
             return carry
-        lax.fori_loop(0, TP, gate_step, 0)
+        for i in range(TP):
+            gate_step(i, 0)
 
     def expand(j, s_buf, du_buf):
         rows = part(j, SUB)
@@ -279,11 +281,13 @@
         m_s[1:, rows, :] = halves(kft, kftl, s_buf, ZROWS)
         dy_s[b, :, rows, :] = halves(kgt, kgtl, du_buf, YROWS)
 
+    bufs = ((sb0, db0), (sb1, db1))
+
     def grid_step(i, b):
-        expand(2 * i + 1, sb1, db1)
-        contract(b, 2 * i, sb0, db0)
-        expand(jnp.minimum(2 * i + 2, GROUPS - 1), sb0, db0)
-        contract(b, 2 * i + 1, sb1, db1)
+        for k in range(UNROLL):
+            j = UNROLL * i + k
+            expand(jnp.minimum(j + 1, GROUPS - 1), *bufs[(k + 1) % 2])
+            contract(b, j, *bufs[k % 2])
         return b
 
     def weight_grads(b, t, lanes):
@@ -400,7 +404,7 @@
     for c in acts(0):
         c.wait_send()
     start(acts(1))
-    per = GROUPS // 2 // TP
+    per = GROUPS // UNROLL // TP
 
     def block_step(b, carry):
         lanes = part(b, BLK)

time: 95.6 us -> 91.7 us (0.959)
  Pallas kernels: 94.9 us -> 90.9 us
    pallas_call x1, Pallas kernels: 92.2 us -> 88.2 us  [step_call(): pl.pallas_call(step_kernel, out_shape=[sds(x.shape, BF16), sds(x.shape, B...]
where the time goes in v8:
time: 91.7 us; the launch traced here: 91.5 us
  Pallas kernels  90.9 us (99%)
    pallas_call x1, Pallas kernels, step_call(): pl.pallas_call(step_kernel, out_shape=[sds(x.shape, BF16), sds(x.shape, B...  88.2 us
    pallas_call x1, Pallas kernels, store_call(): pl.pallas_call(store_kernel, out_shape=[sds(out.shape, BF16), sds(dx.shap...  2.69 us

profile of v8, /device:TPU:3, one launch (start us, length us, event | category | flops | bytes accessed | tf_op | source)
XLA Modules:
  0.0 91.5 jit_solution(10311137336286240920)
XLA Ops:
  0.6 88.2 %step.1 = (bf16[9,32,2048]{2,1,0:T(8,128)(2,1)}, bf16[9,32,2048]{2,1,0:T(8,128)(2,1)}, bf16[896,128]{1,0:T(8,128)(2,1)}) custom-call(bf16[9,32,2048]{2,1,0:T(8,128)(2,1)} %bitcast.5, bf16[9,32,2048]{2,1,0:T(8,128)(2,1)} %bitcast.6, f32[3,32]{1,0:T(4,128)} %gain_loc.1, bf16[3,128,128]{2,1,0:T(8,128)(2,1)} %up_loc.1, bf16[128,128]{1,0:T(8,128)(2,1)} %gate_loc.1, ...), custom_call_target="tpu_custom_call" | custom-call | tf_op jit(solution)/shard_map/step/pallas_call | solution.py:489
  88.9 2.7 %store.1 = (bf16[9,32,2048]{2,1,0:T(8,128)(2,1)}, bf16[9,32,2048]{2,1,0:T(8,128)(2,1)}, bf16[3,128,128]{2,1,0:T(8,128)(2,1)}, bf16[128,128]{1,0:T(8,128)(2,1)}, bf16[3,128,128]{2,1,0:T(8,128)(2,1)}) custom-call(bf16[9,32,2048]{2,1,0:T(8,128)(2,1)} %get-tuple-element.13.out_in, bf16[9,32,2048]{2,1,0:T(8,128)(2,1)} %get-tuple-element.14.dx_in, ...), custom_call_target="tpu_custom_call" | custom-call | tf_op jit(solution)/shard_map/store/pallas_call | solution.py:535

commit v9 on v8

--- a/solution.py
+++ b/solution.py
@@ -77,6 +77,8 @@
 
 
 def degree_of(coef):
+    if isinstance(coef, int):
+        return int(coef >= 1) + int(coef >= TP)
     return jnp.where(coef >= 4, 2, jnp.where(coef >= 1, 1, 0))
 
 
@@ -113,7 +115,7 @@
 
 CHUNK = 288
 KROWS = 144
-UNROLL = 4
+UNROLL = 8
 ZROWS = 64
 YROWS = 72
 GROUPS = HID // SUB
@@ -235,7 +237,8 @@
                 coef = i * DEGS + k
                 y_s[coef] = mm(wup_t[degree_of(coef)], n_s[coef]).astype(BF16)
             return carry
-        lax.fori_loop(0, DEGS, up_step, 0)
+        for i in range(DEGS):
+            up_step(i, 0)
 
     def hidden_grads(b, lanes):
         def grad_step(i, carry):
@@ -243,7 +246,8 @@
                 coef = i * DEGS + k
                 dm_s[coef] = mm(down_all[degree_of(coef)].reshape(HID, CH), g_all[coef, :, lanes]).astype(BF16)
             return carry
-        lax.fori_loop(0, DEGS, grad_step, 0)
+        for i in range(DEGS):
+            grad_step(i, 0)
 
         def gate_step(i, carry):
             rows = part(i, CH)
@@ -306,7 +310,8 @@
                 xk = x_all[coef, :, lanes].astype(F32)
                 out_all[coef, :, lanes] = (xk + mm(wdown_t[degree_of(coef)], m_s[coef])).astype(BF16)
             return carry
-        lax.fori_loop(0, DEGS, down_step, 0)
+        for i in range(DEGS):
+            down_step(i, 0)
 
     def norm_grads(b):
         def norm_grad_step(i, carry):
@@ -314,7 +319,8 @@
                 coef = i * DEGS + k
                 dn_s[coef] = mm(up_all[degree_of(coef)], dy_s[b, coef])
             return carry
-        lax.fori_loop(0, DEGS, norm_grad_step, 0)
+        for i in range(DEGS):
+            norm_grad_step(i, 0)
         dn_s[0] += mm(gate_all[...], da_s[b])
 
     def norm_back(i, carry):

time: 91.7 us -> 90.4 us (0.986)
  Pallas kernels: 90.9 us -> 89.6 us
    pallas_call x1, Pallas kernels: 88.2 us -> 86.9 us  [step_call(): pl.pallas_call(step_kernel, out_shape=[sds(x.shape, BF16), sds(x.shape, B...]
where the time goes in v9:
time: 90.4 us; the launch traced here: 90.2 us
  Pallas kernels  89.6 us (99%)
    pallas_call x1, Pallas kernels, step_call(): pl.pallas_call(step_kernel, out_shape=[sds(x.shape, BF16), sds(x.shape, B...  86.9 us
    pallas_call x1, Pallas kernels, store_call(): pl.pallas_call(store_kernel, out_shape=[sds(out.shape, BF16), sds(dx.shap...  2.69 us

profile of v9, /device:TPU:3, one launch (start us, length us, event | category | flops | bytes accessed | tf_op | source)
XLA Modules:
  0.0 90.2 jit_solution(16867263584053802852)
XLA Ops:
  0.6 86.9 %step.1 = (bf16[9,32,2048]{2,1,0:T(8,128)(2,1)}, bf16[9,32,2048]{2,1,0:T(8,128)(2,1)}, bf16[896,128]{1,0:T(8,128)(2,1)}) custom-call(bf16[9,32,2048]{2,1,0:T(8,128)(2,1)} %bitcast.5, bf16[9,32,2048]{2,1,0:T(8,128)(2,1)} %bitcast.6, f32[3,32]{1,0:T(4,128)} %gain_loc.1, bf16[3,128,128]{2,1,0:T(8,128)(2,1)} %up_loc.1, bf16[128,128]{1,0:T(8,128)(2,1)} %gate_loc.1, ...), custom_call_target="tpu_custom_call" | custom-call | tf_op jit(solution)/shard_map/step/pallas_call | solution.py:495
  87.5 2.7 %store.1 = (bf16[9,32,2048]{2,1,0:T(8,128)(2,1)}, bf16[9,32,2048]{2,1,0:T(8,128)(2,1)}, bf16[3,128,128]{2,1,0:T(8,128)(2,1)}, bf16[128,128]{1,0:T(8,128)(2,1)}, bf16[3,128,128]{2,1,0:T(8,128)(2,1)}) custom-call(bf16[9,32,2048]{2,1,0:T(8,128)(2,1)} %get-tuple-element.13.out_in, bf16[9,32,2048]{2,1,0:T(8,128)(2,1)} %get-tuple-element.14.dx_in, ...), custom_call_target="tpu_custom_call" | custom-call | tf_op jit(solution)/shard_map/store/pallas_call | solution.py:541

commit v10 on v9

--- a/solution.py
+++ b/solution.py
@@ -410,7 +410,6 @@
     for c in acts(0):
         c.wait_send()
     start(acts(1))
-    per = GROUPS // UNROLL // TP
 
     def block_step(b, carry):
         lanes = part(b, BLK)
@@ -422,7 +421,12 @@
         expand(0, sb0, db0)
 
         def quarter_step(t, inner):
-            lax.fori_loop(t * per, (t + 1) * per, grid_step, b)
+            grid_step(t, b)
+            weight_grads(b, t, lanes)
+
+            @pl.when(b == 1)
+            def _():
+                c1(t).start()
 
             @pl.when((b == 1) & (t > 0))
             def _():
@@ -431,11 +435,6 @@
             @pl.when((b == 1) & (t == TP - 1))
             def _():
                 sum_y(0)
-            weight_grads(b, t, lanes)
-
-            @pl.when(b == 1)
-            def _():
-                c1(t).start()
             return inner
         lax.fori_loop(0, TP, quarter_step, 0)
 

time: 90.4 us -> 90.7 us (level)
  no operation moved by 1% of the time
where the time goes in v10:
time: 90.7 us; the launch traced here: 90.5 us
  Pallas kernels  89.9 us (99%)
    pallas_call x1, Pallas kernels, step_call(): pl.pallas_call(step_kernel, out_shape=[sds(x.shape, BF16), sds(x.shape, B...  87.2 us
    pallas_call x1, Pallas kernels, store_call(): pl.pallas_call(store_kernel, out_shape=[sds(out.shape, BF16), sds(dx.shap...  2.69 us

profile of v10, /device:TPU:3, one launch (start us, length us, event | category | flops | bytes accessed | tf_op | source)
XLA Modules:
  0.0 90.5 jit_solution(490518375963159044)
XLA Ops:
  0.6 87.2 %step.1 = (bf16[9,32,2048]{2,1,0:T(8,128)(2,1)}, bf16[9,32,2048]{2,1,0:T(8,128)(2,1)}, bf16[896,128]{1,0:T(8,128)(2,1)}) custom-call(bf16[9,32,2048]{2,1,0:T(8,128)(2,1)} %bitcast.5, bf16[9,32,2048]{2,1,0:T(8,128)(2,1)} %bitcast.6, f32[3,32]{1,0:T(4,128)} %gain_loc.1, bf16[3,128,128]{2,1,0:T(8,128)(2,1)} %up_loc.1, bf16[128,128]{1,0:T(8,128)(2,1)} %gate_loc.1, ...), custom_call_target="tpu_custom_call" | custom-call | tf_op jit(solution)/shard_map/step/pallas_call | solution.py:494
  87.8 2.7 %store.1 = (bf16[9,32,2048]{2,1,0:T(8,128)(2,1)}, bf16[9,32,2048]{2,1,0:T(8,128)(2,1)}, bf16[3,128,128]{2,1,0:T(8,128)(2,1)}, bf16[128,128]{1,0:T(8,128)(2,1)}, bf16[3,128,128]{2,1,0:T(8,128)(2,1)}) custom-call(bf16[9,32,2048]{2,1,0:T(8,128)(2,1)} %get-tuple-element.13.out_in, bf16[9,32,2048]{2,1,0:T(8,128)(2,1)} %get-tuple-element.14.dx_in, ...), custom_call_target="tpu_custom_call" | custom-call | tf_op jit(solution)/shard_map/store/pallas_call | solution.py:540
